TPU v7x, 32 devices: a whole 2x2x4 slice. The times are simulated.
32 devices in a mesh: row: 4 (over z), col: 8 (over y, x, core).
Axes of the slice: x: 2, y: 2, z: 4, core: 2. Of those that a mesh axis runs over, the one named last changes fastest.
Arguments:
- working: float32 [16, 4, 256, 8, 8, 256], P(None, 'row', None, None, 'col'), may hold values from -6 to 6
- factor_panel: float32 [2, 16, 4, 256, 256], P(None, None, 'row'), may hold values from -0.12 to 2, as said below
Outputs:
- gram_part: float32 [16, 4, 256, 8, 8, 256], P(None, 'row', None, None, 'col')
- finished_columns: float32 [8, 4, 256, 8, 4, 512], P(None, None, None, 'col', 'row')
Inputs may be any that keep to these rules, and one draw needn't show every extreme that they name: factor_panel holds a lower-triangular factor: entries above the factor's diagonal are zero and its diagonal entries lie between 1 and 2.
All inputs are finite; a program needn't handle non-finite values.
Results may differ from a plain program's by a relative error of at most 0.0001.
Values sent between devices are 32-bit elements; how exact they have to be, the bound alone decides.
No kernel may reach another device: no remote copies, remote signals or barrier semaphores. Data moves between devices by JAX's collectives and lax.ppermute only.
A program may use at most 256 MiB of HBM per device.

v0:
```python
import jax
import jax.numpy as jnp
from jax import lax
from jax.sharding import PartitionSpec as P

BLK = 256
K = 30
STEPS = 2


def from_root(value, axis, source):
    kept = jnp.where(lax.axis_index(axis) == source, value, 0).astype(value.dtype)
    return lax.psum(kept, axis)


def per_device(working, factor_panel):
    row_count = lax.axis_size("row")
    col_count = lax.axis_size("col")
    row_index = lax.axis_index("row")
    blocks_rows = working.shape[0]
    width = working.shape[2]
    blocks_cols = working.shape[3]
    matrix_rows = working.reshape(blocks_rows, width, blocks_cols * width)
    global_block = jnp.arange(blocks_rows) * row_count + row_index
    solved_list = []
    for step_index in range(STEPS):
        target = K + step_index
        slab = matrix_rows[target // row_count]
        solve_target = K + step_index
        owner = solve_target % row_count
        diagonal = jnp.tril(factor_panel[step_index, solve_target // row_count, 0])
        diagonal = jnp.where(row_index == owner, diagonal, jnp.eye(width, dtype=jnp.float32))
        solve_solved = lax.linalg.triangular_solve(diagonal, slab, left_side=True, lower=True)
        solved = from_root(solve_solved, "row", owner)
        column_part = factor_panel[step_index, :, 0]
        eliminate_target = K + step_index
        updated = matrix_rows - jnp.einsum(
            "rab,bc->rac", column_part, solved, precision=lax.Precision.HIGHEST
        )
        below = (global_block > eliminate_target)[:, None, None]
        here = (global_block == eliminate_target)[:, None, None]
        matrix_rows = jnp.where(below, updated, jnp.where(here, solved[None], matrix_rows))
        solved_list.append(solved)
    stacked = jnp.concatenate(solved_list, 0)
    depth = stacked.shape[0]
    owners_count = col_count // row_count
    pieces = [
        from_root(stacked.reshape(depth, blocks_cols, width), "col", row_index + offset * row_count)
        for offset in range(owners_count)
    ]
    chosen = jnp.stack(pieces, 2)
    row_panels = chosen.reshape(depth, blocks_rows * width)
    gram = lax.dot_general(
        row_panels, stacked, (((0,), (0,)), ((), ())), precision=lax.Precision.HIGHEST
    )
    gram = (gram * (1.0 / (STEPS * BLK))).reshape(blocks_rows, 1, width, blocks_cols, 1, width)
    finished_count = (K + STEPS) // row_count
    finished = matrix_rows[:finished_count].reshape(finished_count, 1, width, 1, row_count, -1)
    moved = lax.all_to_all(finished, "row", split_axis=4, concat_axis=1, tiled=True)
    return (gram, moved)


def solution(mesh):
    placed = (P(None, "row", None, None, "col", None), P(None, None, "row", None, None))
    return jax.shard_map(
        per_device,
        mesh=mesh,
        in_specs=placed,
        out_specs=(
            P(None, "row", None, None, "col", None),
            P(None, None, None, "col", "row", None),
        ),
        check_vma=False,
    )
```

profile of v0, /device:TPU:0, one launch (start us, length us, event | category | flops | bytes accessed | tf_op | source)
XLA Modules:
  0.0 810.9 jit_solution(15085424552516502196)
XLA Ops:
  8.4 4.0 while.4
  12.4 19.7 %custom-call.4 = f32[2,128,128]{1,2,0:T(8,128)S(1)} custom-call(f32[2,128,128]{2,1,0:T(8,128)S(1)} %get-tuple-element.17), custom_call_target="InvertDiagBlocksLowerTriangular" | custom-call | tf_op jit(solution)/shard_map/triangular_solve/custom-call.1 | solution.py:33
  32.1 7.2 slice_reduce_fusion
  44.8 79.1 %copy.24 = f32[16,1,256,8,1,256]{2,5,3,0,4,1:T(8,128)} copy(f32[16,1,256,8,1,256]{5,4,3,2,1,0:T(1,128)} %param.4) | data formatting | bytes 67108864 | tf_op args[0]
  124.0 3.8 while.5
  127.7 19.7 %custom-call.5 = f32[2,128,128]{1,2,0:T(8,128)S(1)} custom-call(f32[2,128,128]{2,1,0:T(8,128)S(1)} %get-tuple-element.18), custom_call_target="InvertDiagBlocksLowerTriangular" | custom-call | tf_op jit(solution)/shard_map/triangular_solve/custom-call.1 | solution.py:33
  147.5 1.9 copy.27
  149.4 73.5 %fusion = f32[16,256,2048]{1,2,0:T(8,128)} fusion(f32[16,256,2048]{1,2,0:T(8,128)} %bitcast.82, f32[256,2048]{0,1:T(8,128)S(1)} %copy.27, pred[16]{0:T(512)(128)(4,1)S(1)} %get-tuple-element.53, pred[16]{0:T(512)(128)(4,1)S(1)} %get-tuple-element.54, f32[2,16,1,256,256]{4,3,1,2,0:T(8,128)} %bitcast.86, f32[256,2048]{1,0:T(8,128)} %all-reduce.5.cloned.1.call-done), kind=kOutput, calls=%fused_computation.5 | convolution fusion | flops 25794969600 | bytes 75497504 | tf_op jit(solution)/shard_map/rab,bc->rac/dot_general | solution.py:37
  225.7 1.8 convolution_subtract_fusion
  230.1 89.0 %all-reduce.7.cloned.1.call-done = f32[256,2048]{1,0:T(8,128)} async-done(((f32[256,2048]{1,0:T(8,128)}), f32[256,2048]{1,0:T(8,128)}) %all-reduce.7.cloned.1.call-update) | async-done | bytes 2097168 | tf_op jit(solution)/shard_map/psum | solution.py:13
  319.2 58.3 %convolution_bitcast_fusion = f32[16,256,2048]{1,2,0:T(8,128)} fusion(f32[2,16,1,256,256]{4,3,1,2,0:T(8,128)} %bitcast.87, f32[256,2048]{1,0:T(8,128)} %all-reduce.7.cloned.1.call-done), kind=kOutput, calls=%fused_computation.6 | convolution fusion | flops 25769803776 | bytes 39845888 | tf_op jit(solution)/shard_map/rab,bc->rac/dot_general | solution.py:37
  377.5 1.8 copy.33
  379.3 18.5 %fusion.1 = f32[8,256,2048]{1,2,0:T(8,128)} fusion(f32[16,256,2048]{1,2,0:T(8,128)} %convolution_bitcast_fusion, f32[16,256,2048]{1,2,0:T(8,128)} %fusion, f32[256,2048]{0,1:T(8,128)} %copy.33, pred[8]{0:T(512)(128)(4,1)S(1)} %bitcast.93, pred[8]{0:T(512)(128)(4,1)S(1)} %bitcast.92), kind=kLoop, calls=%fused_computation.9 | loop fusion | flops 12582912 | bytes 52428816 | tf_op jit(solution)/shard_map/jit(_where)/select_n | solution.py:42
  397.8 16.4 %copy.34 = f32[8,1,256,1,4,512]{5,2,0,3,1,4:T(8,128)} copy(f32[8,1,256,1,4,512]{2,5,4,0,3,1:T(8,128)} %bitcast.83) | data formatting | bytes 33554432 | tf_op jit(solution)/shard_map/reshape | solution.py:58
  414.2 7.2 all-to-all-start
  423.2 4.6 broadcast_select_fusion.1
  427.9 5.4 copy.41
  433.2 5.3 copy.42
  438.6 127.6 %all-reduce.9.cloned.1.call-done = (f32[512,8,1,256]{0,3,2,1:T(8,128)}, f32[512,8,1,256]{0,3,2,1:T(8,128)}) async-done(((f32[512,8,1,256]{0,3,2,1:T(8,128)}, f32[512,8,1,256]{0,3,2,1:T(8,128)}), (f32[512,8,1,256]{0,3,2,1:T(8,128)}, f32[512,8,1,256]{0,3,2,1:T(8,128)})) %all-reduce.9.cloned.1.call-update) | async-done | bytes 8388624 | tf_op jit(solution)/shard_map/psum | solution.py:13
  566.2 4.7 pad_maximum_fusion
  570.9 58.3 %convolution_multiply_fusion = f32[4096,2048]{1,0:T(8,128)} fusion(f32[512,4096]{0,1:T(8,128)S(1)} %bitcast.90, f32[512,2048]{1,0:T(8,128)S(1)} %copy-done.4), kind=kOutput, calls=%fused_computation.7 | convolution fusion | flops 51547996160 | bytes 46137344 | tf_op jit(solution)/shard_map/dot_general | solution.py:53
  629.2 48.3 %reshape.85 = f32[16,1,256,8,1,256]{5,4,3,2,1,0:T(1,128)} reshape(f32[4096,2048]{1,0:T(8,128)} %convolution_multiply_fusion) | data formatting | bytes 67108864 | tf_op jit(solution)/shard_map/reshape | solution.py:56
  677.6 106.6 %all-to-all-done = f32[8,1,256,1,4,512]{5,2,0,3,1,4:T(8,128)} async-done(((f32[8,1,256,1,4,512]{5,2,0,3,1,4:T(8,128)}), f32[8,1,256,1,4,512]{5,2,0,3,1,4:T(8,128)}, u32[]{:S(2)}, u32[]{:S(2)}) %all-to-all-start) | async-done | bytes 16777248 | tf_op jit(solution)/shard_map/all_to_all | solution.py:59
  784.2 19.9 %copy.36 = f32[8,4,256,1,1,512]{5,4,3,2,1,0:T(1,128)} copy(f32[8,4,256,1,1,512]{5,2,0,1,4,3:T(8,128)} %bitcast.22) | data formatting | bytes 33554432
  (47 shorter events, 21.6 us)
Async XLA Ops:
  7.2 140.3 %all-reduce.5.cloned.1.call-start = ((), (), s32[]{:S(2)}) async-start(), calls=%async_computation.1 | async-start | bytes 4194304 | tf_op jit(solution)/shard_map/psum | solution.py:13
  44.8 274.4 %all-reduce.7.cloned.1.call-start = ((), (), s32[]{:S(2)}) async-start(), calls=%async_computation.2 | async-start | bytes 4194304 | tf_op jit(solution)/shard_map/psum | solution.py:13
  319.2 58.3 %copy-start.1 = (f32[256,2048]{1,0:T(8,128)S(1)}, f32[256,2048]{1,0:T(8,128)}, u32[]{:S(2)}) copy-start(f32[256,2048]{1,0:T(8,128)} %all-reduce.7.cloned.1.call-done) | copy-start | bytes 6291460
  414.2 7.3 copy-start
  414.2 370.0 %all-to-all-start = ((f32[8,1,256,1,4,512]{5,2,0,3,1,4:T(8,128)}), f32[8,1,256,1,4,512]{5,2,0,3,1,4:T(8,128)}, u32[]{:S(2)}, u32[]{:S(2)}) async-start(f32[8,1,256,1,4,512]{5,2,0,3,1,4:T(8,128)} %copy.34), calls=%async_computation | async-start | bytes 33554432 | tf_op jit(solution)/shard_map/all_to_all | solution.py:59
  421.4 144.8 %all-reduce.9.cloned.1.call-start = ((), (), s32[]{:S(2)}) async-start(), calls=%async_computation.3 | async-start | bytes 16777216 | tf_op jit(solution)/shard_map/psum | solution.py:13
  421.5 1.6 copy-start.2
  423.2 4.7 copy-start.3
  566.2 4.7 copy-start.4
Sparse Core Ops, SparseCore 0:
  44.9 88.8 all-reduce.4
  230.3 88.8 all-reduce.6
  438.7 127.4 all-reduce.8
where the time goes:
time: 823 us; the launch traced here: 811 us
  waiting for transfers between devices  323 us (39%)
  local copies, waits for them, and re-layouts  197 us (24%)
  matrix products  197 us (24%)
  other arithmetic  71.2 us (9%)
  between operations  14.2 us (2%)
    psum x3, waiting for transfers between devices, from_root(): return lax.psum(kept, axis)  217 us
    dot_general x2, matrix products, per_device(): jnp.einsum('rab,bc->rac', column_part, solved, precision=lax.Precision.HI...  132 us
    all_to_all x1, waiting for transfers between devices, per_device(): lax.all_to_all(finished, 'row', split_axis=4, concat_axis=1, tiled=True)  107 us
    unnamed x14, local copies, waits for them, and re-layouts  102 us
    dot_general x1, matrix products, per_device(): lax.dot_general(row_panels, stacked, (((0,), (0,)), ((), ())), precision=...  58.3 us
    reshape x1, local copies, waits for them, and re-layouts, per_device(): (gram * (1.0 / (STEPS * BLK))).reshape(blocks_rows, 1, width, blocks_cols...  48.3 us
    another operation x4, other arithmetic, per_device(): lax.linalg.triangular_solve(diagonal, slab, left_side=True, lower=True)  40.4 us
    select_n x1, other arithmetic, per_device(): jnp.where(below, updated, jnp.where(here, solved[None], matrix_rows))  18.5 us
  transfers between devices with their start and end apart: 4, of which 3 were waited for; matrix products, arithmetic and copies ran while one was open for 28% of the time, Pallas kernels for 0%

commit v1 on v0

v1 whole, which is shorter than its diff:
```python
import functools

import jax
import jax.numpy as jnp
from jax import lax
from jax.experimental import pallas as pl
from jax.experimental.pallas import tpu as pltpu
from jax.sharding import PartitionSpec as P


K = 30
STEPS = 2
LANES = 128
HIGHEST = lax.Precision.HIGHEST


def copy_block(_, source, target):
    target[...] = source[...]


def copy_into(_, source, __, target):
    target[...] = source[...]


def cost(flops, nbytes):
    return pl.CostEstimate(flops=int(flops), bytes_accessed=int(nbytes), transcendentals=0)


def pack(place, view, first, count):
    _, width, _, group, lanes = view.shape
    return pl.pallas_call(
        copy_block,
        grid_spec=pltpu.PrefetchScalarGridSpec(
            num_scalar_prefetch=1,
            grid=(count,),
            in_specs=[
                pl.BlockSpec((None, width, None, group, lanes), lambda f, at: (f + first, 0, at[0], 0, 0))
            ],
            out_specs=pl.BlockSpec((None, width, group, lanes), lambda f, at: (f, 0, 0, 0)),
        ),
        out_shape=jax.ShapeDtypeStruct((count, width, group, lanes), jnp.float32),
        cost_estimate=cost(0, 2 * 4 * count * width * group * lanes),
        name="pack",
    )(place, view)


def place_own(place, view, count, row_count):
    _, width, _, group, lanes = view.shape
    return pl.pallas_call(
        copy_block,
        grid_spec=pltpu.PrefetchScalarGridSpec(
            num_scalar_prefetch=1,
            grid=(count,),
            in_specs=[pl.BlockSpec((None, width, None, group, lanes), lambda f, at: (f, 0, at[0], 0, 0))],
            out_specs=pl.BlockSpec((None, None, width, group, lanes), lambda f, at: (f, at[0], 0, 0, 0)),
        ),
        out_shape=jax.ShapeDtypeStruct((count, row_count, width, group, lanes), jnp.float32),
        cost_estimate=cost(0, 2 * 4 * count * width * group * lanes),
        name="place_own",
    )(place, view)


def place_piece(place, piece, finished, first):
    count, width, group, lanes = piece.shape
    return pl.pallas_call(
        copy_into,
        grid_spec=pltpu.PrefetchScalarGridSpec(
            num_scalar_prefetch=1,
            grid=(count,),
            in_specs=[
                pl.BlockSpec((None, width, group, lanes), lambda f, at: (f, 0, 0, 0)),
                pl.BlockSpec(memory_space=pl.ANY),
            ],
            out_specs=pl.BlockSpec(
                (None, None, width, group, lanes), lambda f, at: (f + first, at[0], 0, 0, 0)
            ),
        ),
        out_shape=jax.ShapeDtypeStruct(finished.shape, jnp.float32),
        input_output_aliases={2: 0},
        cost_estimate=cost(0, 2 * 4 * piece.size),
        name="place_piece",
    )(place, piece, finished)


def solved_into(_, source, __, target):
    for part in range(target.shape[1]):
        target[:, part, :] = source[:, part * LANES : (part + 1) * LANES]


def place_solved(place, solved, finished, local, owners):
    _, _, width, group, lanes = finished.shape
    first = owners[0]
    return pl.pallas_call(
        solved_into,
        grid_spec=pltpu.PrefetchScalarGridSpec(
            num_scalar_prefetch=1,
            grid=(len(owners),),
            in_specs=[
                pl.BlockSpec((width, group * lanes), lambda s, at: (s, at[0])),
                pl.BlockSpec(memory_space=pl.ANY),
            ],
            out_specs=pl.BlockSpec(
                (None, None, width, group, lanes), lambda s, at: (local, s + first, 0, 0, 0)
            ),
        ),
        out_shape=jax.ShapeDtypeStruct(finished.shape, jnp.float32),
        input_output_aliases={2: 0},
        cost_estimate=cost(0, 2 * 4 * len(owners) * width * group * lanes),
        name="place_solved",
    )(place, solved, finished)


def solved_tile(inverse, source, block, stride, width):
    slabs = []
    for step in range(STEPS):
        halves = [
            source[step, pl.ds(block * (width // LANES) + half, width, stride=stride), :]
            for half in range(width // LANES)
        ]
        slabs.append(jnp.concatenate(halves, 1))
    return jnp.dot(
        inverse[...], jnp.concatenate(slabs, 0), precision=HIGHEST, preferred_element_type=jnp.float32
    )


def split_store(value, high, low):
    top = value.astype(jnp.bfloat16)
    high[...] = top
    low[...] = (value - top.astype(jnp.float32)).astype(jnp.bfloat16)


def solve_local_body(stride, width, inverse, source, solved, high, low):
    value = solved_tile(inverse, source, pl.program_id(0), stride, width)
    solved[...] = value
    split_store(value, high, low)


def solve_local(inverse, slabs, width):
    depth = STEPS * width
    stride = slabs.shape[1] // width
    columns = stride * LANES
    spec = pl.BlockSpec((depth, width), lambda j: (0, j))
    return pl.pallas_call(
        functools.partial(solve_local_body, stride, width),
        grid=(columns // width,),
        in_specs=[
            pl.BlockSpec((depth, depth), lambda j: (0, 0)),
            pl.BlockSpec(slabs.shape, lambda j: (0, 0, 0)),
        ],
        out_specs=[spec, spec, spec],
        out_shape=[
            jax.ShapeDtypeStruct((depth, columns), dtype)
            for dtype in (jnp.float32, jnp.bfloat16, jnp.bfloat16)
        ],
        cost_estimate=cost(12 * depth * depth * columns, 12 * depth * columns),
        name="solve_local",
    )(inverse, slabs)


def solve_panel_body(stride, width, inverse, source, high, low):
    value = solved_tile(inverse, source, pl.program_id(0), stride, width)
    split_store(value.T, high, low)


def solve_panel(inverse, slabs, width):
    depth = STEPS * width
    stride = slabs.shape[1] // width
    blocks = stride * LANES // width
    spec = pl.BlockSpec((None, width, depth), lambda j: (j, 0, 0))
    return pl.pallas_call(
        functools.partial(solve_panel_body, stride, width),
        grid=(blocks,),
        in_specs=[
            pl.BlockSpec((depth, depth), lambda j: (0, 0)),
            pl.BlockSpec(slabs.shape, lambda j: (0, 0, 0)),
        ],
        out_specs=[spec, spec],
        out_shape=[jax.ShapeDtypeStruct((blocks, width, depth), jnp.bfloat16)] * 2,
        cost_estimate=cost(12 * depth * depth * blocks * width, 8 * depth * blocks * width),
        name="solve_panel",
    )(inverse, slabs)


def gram_body(panels, scale, stride, width, *refs):
    panel_refs, (right_high, right_low, out) = refs[: 2 * panels], refs[2 * panels :]
    parts = width // LANES
    for panel in range(panels):
        left_high = panel_refs[2 * panel][...]
        left_low = panel_refs[2 * panel + 1][...]
        for block in range(stride // parts):
            at = slice(block * width, (block + 1) * width)
            high = right_high[:, at]
            total = jnp.dot(left_high, high, preferred_element_type=jnp.float32)
            total += jnp.dot(left_high, right_low[:, at], preferred_element_type=jnp.float32)
            total += jnp.dot(left_low, high, preferred_element_type=jnp.float32)
            total *= scale
            for part in range(parts):
                out[panel, pl.ds(block * parts + part, width, stride=stride), :] = total[
                    :, part * LANES : (part + 1) * LANES
                ]


def gram_product(panel_parts, right_high, right_low, scale):
    panels = len(panel_parts)
    blocks, width, depth = panel_parts[0][0].shape
    columns = right_high.shape[1]
    stride = columns // LANES
    left = pl.BlockSpec((None, width, depth), lambda j: (j, 0, 0))
    right = pl.BlockSpec((depth, columns), lambda j: (0, 0))
    return pl.pallas_call(
        functools.partial(gram_body, panels, scale, stride, width),
        grid=(blocks,),
        in_specs=[left] * (2 * panels) + [right] * 2,
        out_specs=pl.BlockSpec((None, panels, width * stride, LANES), lambda j: (j, 0, 0, 0)),
        out_shape=jax.ShapeDtypeStruct((blocks, panels, width * stride, LANES), jnp.float32),
        cost_estimate=cost(
            6 * depth * panels * blocks * width * columns, 4 * panels * blocks * width * columns
        ),
        name="gram",
    )(*[part for parts in panel_parts for part in parts], right_high, right_low)


def block_inverse(blocks):
    width = blocks[0][0].shape[0]
    eye = jnp.broadcast_to(jnp.eye(width, dtype=jnp.float32), (STEPS, width, width))
    diagonal = jnp.stack([jnp.tril(blocks[s][s]) for s in range(STEPS)])
    inner = lax.linalg.triangular_solve(diagonal, eye, left_side=True, lower=True)
    product = functools.partial(jnp.dot, precision=HIGHEST)
    rows = []
    for row in range(STEPS):
        line = []
        for column in range(STEPS):
            if column > row:
                line.append(jnp.zeros((width, width), jnp.float32))
            elif column == row:
                line.append(inner[row])
            else:
                total = sum(product(blocks[row][k], rows[k][column]) for k in range(column, row))
                line.append(-product(inner[row], total))
        rows.append(line)
    return jnp.concatenate([jnp.concatenate(line, 1) for line in rows], 0)


def window(working, factor_panel):
    row_count = lax.axis_size("row")
    col_count = lax.axis_size("col")
    row = lax.axis_index("row")
    col = lax.axis_index("col")
    blocks_rows, _, width, blocks_cols = working.shape[:4]
    columns = blocks_cols * width
    group = columns // row_count // LANES
    panels = col_count // row_count
    owners = [(K + step) % row_count for step in range(STEPS)]
    finished_count = (K + STEPS) // row_count
    local = finished_count - 1
    plain_rows = [index for index in range(row_count) if index not in owners]

    view = working.reshape(blocks_rows, width, row_count, group, LANES)
    slab = working.reshape(blocks_rows, width * columns // LANES, LANES)[local]

    def shifted(value, shift, senders):
        pairs = [(index, index ^ shift) for index in senders]
        return lax.ppermute(value, "row", pairs)

    part = width // col_count
    slices = lax.dynamic_slice_in_dim(factor_panel[:, local, 0], col * part, part, 1)
    heard = jnp.stack([slices] + [shifted(slices, shift, owners) for shift in range(1, row_count)])
    factor = jnp.stack(
        [lax.dynamic_index_in_dim(heard, row ^ owner, 0, False) for owner in owners]
    )
    size = 1
    while size < col_count:
        other = lax.ppermute(factor, "col", [(index, index ^ size) for index in range(col_count)])
        swap = (col & size) > 0
        factor = jnp.concatenate(
            [jnp.where(swap, other, factor), jnp.where(swap, factor, other)], 2
        )
        size *= 2
    inverse = block_inverse([[factor[s, t] for t in range(STEPS)] for s in range(STEPS)])

    def chain(step_sign):
        held, passed = slab, []
        for hop in range(1, row_count):
            pairs = []
            for owner in owners:
                at = owner + step_sign * hop
                if 0 <= at < row_count:
                    pairs.append((at - step_sign, at))
            if not pairs:
                break
            held = lax.ppermute(held, "row", pairs)
            passed.append(held)
        return passed

    down, up = chain(-1), chain(1)

    def block_row(owner):
        value = slab
        for hop, moved in enumerate(down, 1):
            value = jnp.where(row == owner - hop, moved, value)
        for hop, moved in enumerate(up, 1):
            value = jnp.where(row == owner + hop, moved, value)
        return value

    slabs = jnp.stack([block_row(owner) for owner in owners])

    at = [(row ^ shift).reshape(1) for shift in range(row_count)]
    finished = place_own(at[0], view, finished_count, row_count)
    packed = [pack(at[shift], view, local, 1) for shift in range(1, row_count)]
    last = [shifted(packed[shift - 1], shift, plain_rows) for shift in range(1, row_count)]
    ready = [pack(at[shift], view, 0, local) for shift in range(1, row_count)]
    through = down[-2] if len(down) > 1 else down[-1]
    ready, _ = lax.optimization_barrier((ready, through))
    rest = [shifted(ready[shift - 1], shift, range(row_count)) for shift in range(1, row_count)]

    both = ("row", "col")
    low_place = lax.rem(col, row_count)
    high_place = col // row_count

    def joined(value, holds, target):
        pairs = []
        for r in range(row_count):
            for c in range(col_count):
                if holds((c % row_count) ^ r):
                    pairs.append((r * col_count + c, r * col_count + target(c)))
        return lax.ppermute(value, both, pairs)

    held_bits = 0
    held = slabs
    bit = row_count // 2
    while bit > 1:
        moved = joined(held, lambda d, b=held_bits: d & ~b == 0, lambda c, b=bit: c ^ b)
        held = jnp.where((low_place ^ row) & bit > 0, moved, held)
        held_bits |= bit
        bit //= 2
    parts = [held]
    for shift in range(1, panels):
        parts.append(joined(held, lambda d: d & ~held_bits == 0, lambda c, s=shift: (c + s * row_count) % col_count))
    if row_count > 1:
        near = (low_place ^ row) & 1 > 0
        parts = [
            jnp.where(near, joined(value, lambda d: d & ~held_bits == 0, lambda c: c ^ 1), value)
            for value in parts
        ]
    panel_slabs = []
    for place in range(panels):
        value = parts[0]
        for shift in range(1, panels):
            value = jnp.where(lax.rem(high_place - place + panels, panels) == shift, parts[shift], value)
        panel_slabs.append(value)

    solved, right_high, right_low = solve_local(inverse, slabs, width)
    panel_parts = [solve_panel(inverse, value, width) for value in panel_slabs]
    gram = gram_product(panel_parts, right_high, right_low, 1.0 / (STEPS * width))

    for shift in range(1, row_count):
        finished = place_piece(at[shift], last[shift - 1], finished, local)
    finished = place_solved(at[0], solved, finished, local, owners)
    for shift in send_order(row_count):
        finished = place_piece(at[shift], rest[shift - 1], finished, 0)

    return (
        gram.reshape(working.shape),
        finished.reshape(finished_count, row_count, width, 1, 1, group * LANES),
    )


def send_order(row_count):
    return sorted(range(1, row_count), key=lambda shift: (shift == row_count - 1, -(shift & (row_count // 2)), shift))


def solution(mesh):
    return jax.shard_map(
        window,
        mesh=mesh,
        in_specs=(P(None, "row", None, None, "col", None), P(None, None, "row", None, None)),
        out_specs=(
            P(None, "row", None, None, "col", None),
            P(None, None, None, "col", "row", None),
        ),
        check_vma=False,
    )
```

time: 823 us -> 689 us (0.84)
  the two profiles are of different devices: /device:TPU:0 before, /device:TPU:24 now
where the time goes in v1:
time: 689 us; the launch traced here: 687 us
  waiting for transfers between devices  342 us (50%)
  Pallas kernels  137 us (20%)
  starting transfers between devices  133 us (19%)
  other arithmetic  63.9 us (9%)
  local copies, waits for them, and re-layouts  8.54 us (1%)
    ppermute x9, waiting for transfers between devices, shifted(): return lax.ppermute(value, 'row', pairs)  249 us
    ppermute x9, starting transfers between devices, shifted(): return lax.ppermute(value, 'row', pairs)  113 us
    ppermute x4, waiting for transfers between devices, chain(): held = lax.ppermute(held, 'row', pairs)  91.4 us
    another operation x4, other arithmetic, block_inverse(): lax.linalg.triangular_solve(diagonal, eye, left_side=True, lower=True)  39.4 us
    pallas_call x1, Pallas kernels, gram_product(): pl.pallas_call(functools.partial(gram_body, panels, scale, stride, width)...  39.4 us
    pallas_call x2, Pallas kernels, solve_panel(): pl.pallas_call(functools.partial(solve_panel_body, stride, width), grid=(...  27.6 us
    pallas_call x6, Pallas kernels, place_piece(): pl.pallas_call(copy_into, grid_spec=pltpu.PrefetchScalarGridSpec(num_scal...  23.8 us
    pallas_call x6, Pallas kernels, pack(): pl.pallas_call(copy_block, grid_spec=pltpu.PrefetchScalarGridSpec(num_sca...  23.7 us
  transfers between devices with their start and end apart: 20, of which 7 were waited for; matrix products, arithmetic and copies ran while one was open for 7% of the time, Pallas kernels for 10%

profile of v1, /device:TPU:24, one launch (start us, length us, event | category | flops | bytes accessed | tf_op | source)
XLA Modules:
  0.0 687.2 jit_solution(7841607940819022658)
XLA Ops:
  6.2 44.7 %collective-permute-done.7 = f32[4096,128]{1,0:T(8,128)S(1)} collective-permute-done((f32[4096,128]{1,0:T(8,128)S(1)}, f32[4096,128]{1,0:T(8,128)S(1)}, u32[]{:S(2)}, u32[]{:S(2)}) %collective-permute-start.7) | collective-permute-done | bytes 2097184 | tf_op jit(solution)/shard_map/ppermute | solution.py:291
  57.6 46.7 %collective-permute-done.6 = f32[4096,128]{1,0:T(8,128)} collective-permute-done((f32[4096,128]{1,0:T(8,128)S(1)}, f32[4096,128]{1,0:T(8,128)}, u32[]{:S(2)}, u32[]{:S(2)}) %collective-permute-start.6) | collective-permute-done | bytes 2097184 | tf_op jit(solution)/shard_map/ppermute | solution.py:291
  104.2 4.6 select_bitcast_fusion.1
  114.2 5.3 broadcast_select_fusion.1
  122.2 50.1 %collective-permute-start = (f32[2,32,256]{2,1,0:T(8,128)S(1)}, f32[2,32,256]{2,1,0:T(8,128)S(1)}, u32[]{:S(2)}, u32[]{:S(2)}) collective-permute-start(f32[2,32,256]{2,1,0:T(8,128)S(1)} %get-tuple-element.55), channel_id=1, source_target_pairs={{16,24},{24,16},{17,25},{25,17},{18,26},{26,18},{19,27},{27,19},{2... | collective-permute-start | bytes 196616 | tf_op jit(solution)/shard_map/ppermute | solution.py:263
  173.7 45.7 %collective-permute-start.2 = (f32[2,32,256]{2,1,0:T(8,128)S(1)}, f32[2,32,256]{2,1,0:T(8,128)S(1)}, u32[]{:S(2)}, u32[]{:S(2)}) collective-permute-start(f32[2,32,256]{2,1,0:T(8,128)S(1)} %get-tuple-element.55), channel_id=1, source_target_pairs={{16,8},{24,0},{17,9},{25,1},{18,10},{26,2},{19,11},{27,3},{20,12},... | collective-permute-start | bytes 196616 | tf_op jit(solution)/shard_map/ppermute | solution.py:263
  239.7 6.0 pack.7
  245.7 6.0 pack.8
  251.8 6.0 pack.6
  257.9 94.5 %collective-permute-done.18.source = f32[1,256,4,128]{3,2,1,0:T(4,128)S(1)} collective-permute-done((f32[1,256,4,128]{3,2,1,0:T(4,128)}, f32[1,256,4,128]{3,2,1,0:T(4,128)S(1)}, u32[]{:S(2)}, u32[]{:S(2)}) %collective-permute-start.18) | collective-permute-done | bytes 524320 | tf_op jit(solution)/shard_map/ppermute | solution.py:263
  352.4 11.8 %collective-permute-start.15 = (f32[7,256,4,128]{3,2,1,0:T(4,128)}, f32[7,256,4,128]{3,2,1,0:T(4,128)}, u32[]{:S(2)}, u32[]{:S(2)}) collective-permute-start(f32[7,256,4,128]{3,2,1,0:T(4,128)} %pack.6), channel_id=1, source_target_pairs={{0,8},{8,0},{16,24},{24,16},{1,9},{9,1},{17,25},{25,17},{2,10},{10... | collective-permute-start | bytes 11010056 | tf_op jit(solution)/shard_map/ppermute | solution.py:263
  364.7 6.6 place_own.1.__
  377.2 3.9 while.1
  381.1 39.3 %custom-call.3 = f32[2,2,128,128]{2,3,1,0:T(8,128)S(1)} custom-call(f32[2,2,128,128]{3,2,1,0:T(8,128)S(1)} %bitcast.72), custom_call_target="InvertDiagBlocksLowerTriangular" | custom-call | tf_op jit(solution)/shard_map/triangular_solve | solution.py:227
  423.6 13.6 %solve_local.1 = (f32[512,2048]{1,0:T(8,128)}, bf16[512,2048]{1,0:T(8,128)(2,1)}, bf16[512,2048]{1,0:T(8,128)(2,1)}) custom-call(f32[512,512]{1,0:T(8,128)} %select_maximum_fusion.inverse, f32[2,4096,128]{2,1,0:T(8,128)} %pad_maximum_fusion.source), custom_call_target="tpu_custom_call" | custom-call | flops 6442450944 | bytes 12582912 | tf_op jit(solution)/shard_map/solve_local/pallas_call | solution.py:143
  439.6 81.4 %collective-permute-done.16.source = f32[7,256,4,128]{3,2,1,0:T(4,128)} collective-permute-done((f32[7,256,4,128]{3,2,1,0:T(4,128)}, f32[7,256,4,128]{3,2,1,0:T(4,128)}, u32[]{:S(2)}, u32[]{:S(2)}) %collective-permute-start.16) | collective-permute-done | bytes 3670048 | tf_op jit(solution)/shard_map/ppermute | solution.py:263
  521.0 6.0 place_piece.9.__
  527.0 71.3 %collective-permute-done.15.source = f32[7,256,4,128]{3,2,1,0:T(4,128)} collective-permute-done((f32[7,256,4,128]{3,2,1,0:T(4,128)}, f32[7,256,4,128]{3,2,1,0:T(4,128)}, u32[]{:S(2)}, u32[]{:S(2)}) %collective-permute-start.15) | collective-permute-done | bytes 3670048 | tf_op jit(solution)/shard_map/ppermute | solution.py:263
  598.3 6.0 place_piece.10.__
  604.3 6.2 place_piece.11
  610.5 9.8 %broadcast_select_fusion = (f32[2,4096,128]{2,1,0:T(8,128)}, f32[2,4096,128]{2,1,0:T(8,128)}) fusion(pred[]{:T(512)S(6)} %eq.39, f32[2,4096,128]{2,1,0:T(8,128)} %collective-permute-done.12, f32[2,4096,128]{2,1,0:T(8,128)} %collective-permute-done.11, pred[]{:T(512)S(6)} %gt.18, f32[2,4096,128]{2,1,0:T(8,128)} %collective-permute-done.13, pred[]{:T(512)S(6)} %eq.32, ...), kind=kLoop, calls=%fused_computation.5 | loop fusion | flops 6291456 | bytes 29360132 | tf_op jit(solution)/shard_map/jit(_where)/select_n | solution.py:349
  620.2 13.8 %solve_panel.3 = (bf16[8,256,512]{2,1,0:T(8,128)(2,1)}, bf16[8,256,512]{2,1,0:T(8,128)(2,1)}) custom-call(f32[512,512]{1,0:T(8,128)} %select_maximum_fusion.inverse, f32[2,4096,128]{2,1,0:T(8,128)} %get-tuple-element.42.source), custom_call_target="tpu_custom_call" | custom-call | flops 6442450944 | bytes 8388608 | tf_op jit(solution)/shard_map/solve_panel/pallas_call | solution.py:170
  634.1 13.8 %solve_panel.2 = (bf16[8,256,512]{2,1,0:T(8,128)(2,1)}, bf16[8,256,512]{2,1,0:T(8,128)(2,1)}) custom-call(f32[512,512]{1,0:T(8,128)} %select_maximum_fusion.inverse, f32[2,4096,128]{2,1,0:T(8,128)} %get-tuple-element.43.source), custom_call_target="tpu_custom_call" | custom-call | flops 6442450944 | bytes 8388608 | tf_op jit(solution)/shard_map/solve_panel/pallas_call | solution.py:170
  647.8 39.4 %gram.1 = f32[8,2,4096,128]{3,2,1,0:T(8,128)} custom-call(bf16[8,256,512]{2,1,0:T(8,128)(2,1)} %get-tuple-element.12.refs_0_, bf16[8,256,512]{2,1,0:T(8,128)(2,1)} %get-tuple-element.13.refs_1_, bf16[8,256,512]{2,1,0:T(8,128)(2,1)} %get-tuple-element.14.refs_2_, bf16[8,256,512]{2,1,0:T(8,128)(2,1)} %get-tuple-element.15.refs_3_, ...), custom_call_target="tpu_custom_call" | custom-call | flops 25769803776 | bytes 33554432 | tf_op jit(solution)/shard_map/gram/pallas_call | solution.py:210
  (89 shorter events, 57.6 us)
Async XLA Ops:
  3.7 100.6 %copy-start.3 = (f32[1,1,256,8,1,256]{5,4,3,2,1,0:T(1,128)}, f32[1,1,256,8,1,256]{5,4,3,2,1,0:T(1,128)S(1)}, u32[]{:S(2)}) copy-start(f32[1,1,256,8,1,256]{5,4,3,2,1,0:T(1,128)S(1)} %slice.41) | copy-start | bytes 6291460
  3.7 47.2 %collective-permute-start.7 = (f32[4096,128]{1,0:T(8,128)S(1)}, f32[4096,128]{1,0:T(8,128)S(1)}, u32[]{:S(2)}, u32[]{:S(2)}) collective-permute-start(f32[4096,128]{1,0:T(8,128)S(1)} %bitcast.66), channel_id=1, source_target_pairs={{16,8},{24,16},{17,9},{25,17},{18,10},{26,18},{19,11},{27,19},{20,... | collective-permute-start | bytes 6291464 | tf_op jit(solution)/shard_map/ppermute | solution.py:291
  52.2 3.3 collective-permute-start.8
  54.2 50.0 %collective-permute-start.6 = (f32[4096,128]{1,0:T(8,128)S(1)}, f32[4096,128]{1,0:T(8,128)}, u32[]{:S(2)}, u32[]{:S(2)}) collective-permute-start(f32[4096,128]{1,0:T(8,128)S(1)} %bitcast.67), channel_id=1, source_target_pairs={{16,24},{17,25},{18,26},{19,27},{20,28},{21,29},{22,30},{23,31}} | collective-permute-start | bytes 6291464 | tf_op jit(solution)/shard_map/ppermute | solution.py:291
  55.5 48.7 %collective-permute-start.9 = (f32[4096,128]{1,0:T(8,128)}, f32[4096,128]{1,0:T(8,128)}, u32[]{:S(2)}, u32[]{:S(2)}) collective-permute-start(f32[4096,128]{1,0:T(8,128)} %collective-permute-done.8), channel_id=1, source_target_pairs={{8,0},{9,1},{10,2},{11,3},{12,4},{13,5},{14,6},{15,7}} | collective-permute-start | bytes 6291464 | tf_op jit(solution)/shard_map/ppermute | solution.py:291
  111.6 2.6 collective-permute-start.10
  119.5 118.7 %collective-permute-start.11 = (f32[2,4096,128]{2,1,0:T(8,128)}, f32[2,4096,128]{2,1,0:T(8,128)}, u32[]{:S(2)}, u32[]{:S(2)}) collective-permute-start(f32[2,4096,128]{2,1,0:T(8,128)} %broadcast_select_fusion.1), channel_id=1, source_target_pairs={{0,4},{2,6},{4,0},{6,2},{9,13},{11,15},{13,9},{15,11},{16,20},{18,... | collective-permute-start | bytes 12582920 | tf_op jit(solution)/shard_map/ppermute | solution.py:326
  122.2 97.1 %collective-permute-start = (f32[2,32,256]{2,1,0:T(8,128)S(1)}, f32[2,32,256]{2,1,0:T(8,128)S(1)}, u32[]{:S(2)}, u32[]{:S(2)}) collective-permute-start(f32[2,32,256]{2,1,0:T(8,128)S(1)} %get-tuple-element.55), channel_id=1, source_target_pairs={{16,24},{24,16},{17,25},{25,17},{18,26},{26,18},{19,27},{27,19},{2... | collective-permute-start | bytes 196616 | tf_op jit(solution)/shard_map/ppermute | solution.py:263
  172.4 47.0 %collective-permute-start.1 = (f32[2,32,256]{2,1,0:T(8,128)S(1)}, f32[2,32,256]{2,1,0:T(8,128)S(1)}, u32[]{:S(2)}, u32[]{:S(2)}) collective-permute-start(f32[2,32,256]{2,1,0:T(8,128)S(1)} %get-tuple-element.55), channel_id=1, source_target_pairs={{16,0},{24,8},{17,1},{25,9},{18,2},{26,10},{19,3},{27,11},{20,4},{... | collective-permute-start | bytes 196616 | tf_op jit(solution)/shard_map/ppermute | solution.py:263
  173.7 47.6 %collective-permute-start.2 = (f32[2,32,256]{2,1,0:T(8,128)S(1)}, f32[2,32,256]{2,1,0:T(8,128)S(1)}, u32[]{:S(2)}, u32[]{:S(2)}) collective-permute-start(f32[2,32,256]{2,1,0:T(8,128)S(1)} %get-tuple-element.55), channel_id=1, source_target_pairs={{16,8},{24,0},{17,9},{25,1},{18,10},{26,2},{19,11},{27,3},{20,12},... | collective-permute-start | bytes 196616 | tf_op jit(solution)/shard_map/ppermute | solution.py:263
  221.3 1.4 collective-permute-start.3
  222.8 12.8 %collective-permute-start.4 = (f32[2,2,64,256]{3,2,1,0:T(8,128)S(1)}, f32[2,2,64,256]{3,2,1,0:T(8,128)S(1)}, u32[]{:S(2)}, u32[]{:S(2)}) collective-permute-start(f32[2,2,64,256]{3,2,1,0:T(8,128)S(1)} %pad_maximum_fusion.5), channel_id=1, source_target_pairs={{0,2},{1,3},{2,0},{3,1},{4,6},{5,7},{6,4},{7,5},{8,10},{9,11},{10,... | collective-permute-start | bytes 786440 | tf_op jit(solution)/shard_map/ppermute | solution.py:273
  228.5 8.5 %collective-permute-start.19 = (f32[1,256,4,128]{3,2,1,0:T(4,128)}, f32[1,256,4,128]{3,2,1,0:T(4,128)S(1)}, u32[]{:S(2)}, u32[]{:S(2)}) collective-permute-start(f32[1,256,4,128]{3,2,1,0:T(4,128)} %pack.11), channel_id=1, source_target_pairs={{0,8},{8,0},{1,9},{9,1},{2,10},{10,2},{3,11},{11,3},{4,12},{12,4},... | collective-permute-start | bytes 1572872 | tf_op jit(solution)/shard_map/ppermute | solution.py:263
  231.1 121.3 %collective-permute-start.18 = (f32[1,256,4,128]{3,2,1,0:T(4,128)}, f32[1,256,4,128]{3,2,1,0:T(4,128)S(1)}, u32[]{:S(2)}, u32[]{:S(2)}) collective-permute-start(f32[1,256,4,128]{3,2,1,0:T(4,128)} %pack.10), channel_id=1, source_target_pairs={{0,16},{8,24},{1,17},{9,25},{2,18},{10,26},{3,19},{11,27},{4,20},{... | collective-permute-start | bytes 1572872 | tf_op jit(solution)/shard_map/ppermute | solution.py:263
  234.3 118.1 %collective-permute-start.17 = (f32[1,256,4,128]{3,2,1,0:T(4,128)}, f32[1,256,4,128]{3,2,1,0:T(4,128)S(1)}, u32[]{:S(2)}, u32[]{:S(2)}) collective-permute-start(f32[1,256,4,128]{3,2,1,0:T(4,128)} %pack.9), channel_id=1, source_target_pairs={{0,24},{8,16},{1,25},{9,17},{2,26},{10,18},{3,27},{11,19},{4,28},{... | collective-permute-start | bytes 1572872 | tf_op jit(solution)/shard_map/ppermute | solution.py:263
  236.5 127.7 %collective-permute-start.5 = (f32[2,2,128,256]{3,2,1,0:T(8,128)}, f32[2,2,128,256]{3,2,1,0:T(8,128)S(1)}, u32[]{:S(2)}, u32[]{:S(2)}) collective-permute-start(f32[2,2,128,256]{3,2,1,0:T(8,128)} %pad_maximum_fusion.1), channel_id=1, source_target_pairs={{0,4},{1,5},{2,6},{3,7},{4,0},{5,1},{6,2},{7,3},{8,12},{9,13},{10,... | collective-permute-start | bytes 1572872 | tf_op jit(solution)/shard_map/ppermute | solution.py:273
  237.0 8.8 %copy-start.5 = (f32[1,256,4,128]{3,2,1,0:T(4,128)}, f32[1,256,4,128]{3,2,1,0:T(4,128)S(1)}, u32[]{:S(2)}) copy-start(f32[1,256,4,128]{3,2,1,0:T(4,128)S(1)} %collective-permute-done.19.source) | copy-start | bytes 1572868
  237.0 373.5 %collective-permute-start.13 = (f32[2,4096,128]{2,1,0:T(8,128)}, f32[2,4096,128]{2,1,0:T(8,128)}, u32[]{:S(2)}, u32[]{:S(2)}) collective-permute-start(f32[2,4096,128]{2,1,0:T(8,128)} %broadcast_select_fusion.1), channel_id=1, source_target_pairs={{0,1},{2,3},{4,5},{6,7},{9,8},{11,10},{13,12},{15,14},{16,17},{18,... | collective-permute-start | bytes 12582920 | tf_op jit(solution)/shard_map/ppermute | solution.py:326
  238.3 372.2 %collective-permute-start.12 = (f32[2,4096,128]{2,1,0:T(8,128)}, f32[2,4096,128]{2,1,0:T(8,128)}, u32[]{:S(2)}, u32[]{:S(2)}) collective-permute-start(f32[2,4096,128]{2,1,0:T(8,128)} %collective-permute-done.11), channel_id=1, source_target_pairs={{0,1},{2,3},{4,5},{6,7},{9,8},{11,10},{13,12},{15,14},{16,17},{18,... | collective-permute-start | bytes 12582920 | tf_op jit(solution)/shard_map/ppermute | solution.py:326
  352.4 19.0 %copy-start.6 = (f32[1,256,4,128]{3,2,1,0:T(4,128)}, f32[1,256,4,128]{3,2,1,0:T(4,128)S(1)}, u32[]{:S(2)}) copy-start(f32[1,256,4,128]{3,2,1,0:T(4,128)S(1)} %collective-permute-done.18.source) | copy-start | bytes 1572868
  352.4 168.7 %collective-permute-start.16 = (f32[7,256,4,128]{3,2,1,0:T(4,128)}, f32[7,256,4,128]{3,2,1,0:T(4,128)}, u32[]{:S(2)}, u32[]{:S(2)}) collective-permute-start(f32[7,256,4,128]{3,2,1,0:T(4,128)} %pack.7), channel_id=1, source_target_pairs={{0,16},{8,24},{16,0},{24,8},{1,17},{9,25},{17,1},{25,9},{2,18},{10... | collective-permute-start | bytes 11010056 | tf_op jit(solution)/shard_map/ppermute | solution.py:263
  352.4 18.9 %copy-start.7 = (f32[1,256,4,128]{3,2,1,0:T(4,128)}, f32[1,256,4,128]{3,2,1,0:T(4,128)S(1)}, u32[]{:S(2)}) copy-start(f32[1,256,4,128]{3,2,1,0:T(4,128)S(1)} %collective-permute-done.17.source) | copy-start | bytes 1572868
  352.4 245.9 %collective-permute-start.15 = (f32[7,256,4,128]{3,2,1,0:T(4,128)}, f32[7,256,4,128]{3,2,1,0:T(4,128)}, u32[]{:S(2)}, u32[]{:S(2)}) collective-permute-start(f32[7,256,4,128]{3,2,1,0:T(4,128)} %pack.6), channel_id=1, source_target_pairs={{0,8},{8,0},{16,24},{24,16},{1,9},{9,1},{17,25},{25,17},{2,10},{10... | collective-permute-start | bytes 11010056 | tf_op jit(solution)/shard_map/ppermute | solution.py:263
  364.2 240.2 %collective-permute-start.14 = (f32[7,256,4,128]{3,2,1,0:T(4,128)}, f32[7,256,4,128]{3,2,1,0:T(4,128)}, u32[]{:S(2)}, u32[]{:S(2)}) collective-permute-start(f32[7,256,4,128]{3,2,1,0:T(4,128)} %pack.8), channel_id=1, source_target_pairs={{0,24},{8,16},{16,8},{24,0},{1,25},{9,17},{17,9},{25,1},{2,26},{10... | collective-permute-start | bytes 11010056 | tf_op jit(solution)/shard_map/ppermute | solution.py:263
  (5 other events, 23.5 us)

commit v2 on v1

--- a/solution.py
+++ b/solution.py
@@ -10,6 +10,7 @@
 
 K = 30
 STEPS = 2
+PARTS = 2
 LANES = 128
 HIGHEST = lax.Precision.HIGHEST
 
@@ -80,6 +81,39 @@
         cost_estimate=cost(0, 2 * 4 * piece.size),
         name="place_piece",
     )(place, piece, finished)
+
+
+def either_into(at, one, other, _, target):
+    @pl.when(at[1] > 0)
+    def _():
+        target[...] = one[...]
+
+    @pl.when(at[1] == 0)
+    def _():
+        target[...] = other[...]
+
+
+def place_either(place, one, other, finished, first):
+    count, width, group, lanes = one.shape
+    return pl.pallas_call(
+        either_into,
+        grid_spec=pltpu.PrefetchScalarGridSpec(
+            num_scalar_prefetch=1,
+            grid=(count,),
+            in_specs=[
+                pl.BlockSpec((None, width, group, lanes), lambda f, at: (f * at[1], 0, 0, 0)),
+                pl.BlockSpec((None, width, group, lanes), lambda f, at: (f * (1 - at[1]), 0, 0, 0)),
+                pl.BlockSpec(memory_space=pl.ANY),
+            ],
+            out_specs=pl.BlockSpec(
+                (None, None, width, group, lanes), lambda f, at: (f + first, at[0], 0, 0, 0)
+            ),
+        ),
+        out_shape=jax.ShapeDtypeStruct(finished.shape, jnp.float32),
+        input_output_aliases={3: 0},
+        cost_estimate=cost(0, 2 * 4 * one.size),
+        name="place_either",
+    )(place, one, other, finished)
 
 
 def solved_into(_, source, __, target):
@@ -256,15 +290,36 @@
     plain_rows = [index for index in range(row_count) if index not in owners]
 
     view = working.reshape(blocks_rows, width, row_count, group, LANES)
-    slab = working.reshape(blocks_rows, width * columns // LANES, LANES)[local]
+    slab_rows = width * columns // LANES // PARTS
+    slab_parts = working.reshape(blocks_rows, PARTS, slab_rows, LANES)
+    slab = [slab_parts[local, part] for part in range(PARTS)]
 
     def shifted(value, shift, senders):
         pairs = [(index, index ^ shift) for index in senders]
         return lax.ppermute(value, "row", pairs)
 
+    def chain(step_sign, part):
+        held, passed = slab[part], []
+        for hop in range(1, row_count):
+            pairs = []
+            for owner in owners:
+                at = owner + step_sign * hop
+                if 0 <= at < row_count:
+                    pairs.append((at - step_sign, at))
+            if not pairs:
+                break
+            held = lax.ppermute(held, "row", pairs)
+            passed.append(held)
+        return passed
+
+    down = [chain(-1, part) for part in range(PARTS)]
+    up = [chain(1, part) for part in range(PARTS)]
+
     part = width // col_count
     slices = lax.dynamic_slice_in_dim(factor_panel[:, local, 0], col * part, part, 1)
-    heard = jnp.stack([slices] + [shifted(slices, shift, owners) for shift in range(1, row_count)])
+    heard = [slices] + [shifted(slices, shift, owners) for shift in range(1, row_count)]
+    heard, _ = lax.optimization_barrier((heard, down[-1][0]))
+    heard = jnp.stack(heard)
     factor = jnp.stack(
         [lax.dynamic_index_in_dim(heard, row ^ owner, 0, False) for owner in owners]
     )
@@ -278,40 +333,36 @@
         size *= 2
     inverse = block_inverse([[factor[s, t] for t in range(STEPS)] for s in range(STEPS)])
 
-    def chain(step_sign):
-        held, passed = slab, []
-        for hop in range(1, row_count):
-            pairs = []
-            for owner in owners:
-                at = owner + step_sign * hop
-                if 0 <= at < row_count:
-                    pairs.append((at - step_sign, at))
-            if not pairs:
-                break
-            held = lax.ppermute(held, "row", pairs)
-            passed.append(held)
-        return passed
-
-    down, up = chain(-1), chain(1)
-
-    def block_row(owner):
-        value = slab
-        for hop, moved in enumerate(down, 1):
+    def block_row(owner, part):
+        value = slab[part]
+        for hop, moved in enumerate(down[part], 1):
             value = jnp.where(row == owner - hop, moved, value)
-        for hop, moved in enumerate(up, 1):
+        for hop, moved in enumerate(up[part], 1):
             value = jnp.where(row == owner + hop, moved, value)
         return value
 
-    slabs = jnp.stack([block_row(owner) for owner in owners])
+    slabs = jnp.stack(
+        [jnp.concatenate([block_row(owner, part) for part in range(PARTS)], 0) for owner in owners]
+    )
 
     at = [(row ^ shift).reshape(1) for shift in range(row_count)]
     finished = place_own(at[0], view, finished_count, row_count)
     packed = [pack(at[shift], view, local, 1) for shift in range(1, row_count)]
     last = [shifted(packed[shift - 1], shift, plain_rows) for shift in range(1, row_count)]
-    ready = [pack(at[shift], view, 0, local) for shift in range(1, row_count)]
-    through = down[-2] if len(down) > 1 else down[-1]
-    ready, _ = lax.optimization_barrier((ready, through))
-    rest = [shifted(ready[shift - 1], shift, range(row_count)) for shift in range(1, row_count)]
+    ready = {
+        (shift, first): pack(at[shift], view, first, count)
+        for shift in range(1, row_count)
+        for first, count in pieces(shift, row_count, local)
+    }
+    middle = row_count // 2
+    inner = [middle - 1, middle]
+    outer = [index for index in range(row_count) if index not in inner]
+    rest = {}
+    for (shift, first), value in ready.items():
+        if shift == middle:
+            rest[shift, first] = (shifted(value, shift, inner), shifted(value, shift, outer))
+        else:
+            rest[shift, first] = (shifted(value, shift, range(row_count)),)
 
     both = ("row", "col")
     low_place = lax.rem(col, row_count)
@@ -356,8 +407,18 @@
     for shift in range(1, row_count):
         finished = place_piece(at[shift], last[shift - 1], finished, local)
     finished = place_solved(at[0], solved, finished, local, owners)
+    from_inner = ((row ^ middle) == inner[0]) | ((row ^ middle) == inner[1])
     for shift in send_order(row_count):
-        finished = place_piece(at[shift], rest[shift - 1], finished, 0)
+        for first, _ in pieces(shift, row_count, local):
+            if shift == middle:
+                finished = place_either(
+                    jnp.concatenate([at[shift], from_inner.astype(jnp.int32).reshape(1)]),
+                    *rest[shift, first],
+                    finished,
+                    first,
+                )
+            else:
+                finished = place_piece(at[shift], *rest[shift, first], finished, first)
 
     return (
         gram.reshape(working.shape),
@@ -367,6 +428,13 @@
 
 def send_order(row_count):
     return sorted(range(1, row_count), key=lambda shift: (shift == row_count - 1, -(shift & (row_count // 2)), shift))
+
+
+def pieces(shift, row_count, count):
+    small = max(count // 4, 1)
+    if shift == row_count - 1 and count > small:
+        return [(0, count - small), (count - small, small)]
+    return [(0, count)]
 
 
 def solution(mesh):

time: 689 us -> 653 us (0.948)
  the two profiles are of different devices: /device:TPU:24 before, /device:TPU:10 now
where the time goes in v2:
time: 653 us; the launch traced here: 651 us
  waiting for transfers between devices  394 us (60%)
  Pallas kernels  140 us (21%)
  other arithmetic  64.4 us (10%)
  starting transfers between devices  42 us (6%)
  local copies, waits for them, and re-layouts  6.63 us (1%)
    ppermute x11, waiting for transfers between devices, shifted(): return lax.ppermute(value, 'row', pairs)  289 us
    ppermute x8, waiting for transfers between devices, chain(): held = lax.ppermute(held, 'row', pairs)  104 us
    another operation x4, other arithmetic, block_inverse(): lax.linalg.triangular_solve(diagonal, eye, left_side=True, lower=True)  39.4 us
    pallas_call x1, Pallas kernels, gram_product(): pl.pallas_call(functools.partial(gram_body, panels, scale, stride, width)...  39.4 us
    pallas_call x2, Pallas kernels, solve_panel(): pl.pallas_call(functools.partial(solve_panel_body, stride, width), grid=(...  27.6 us
    pallas_call x7, Pallas kernels, pack(): pl.pallas_call(copy_block, grid_spec=pltpu.PrefetchScalarGridSpec(num_sca...  25 us
    ppermute x11, starting transfers between devices, shifted(): return lax.ppermute(value, 'row', pairs)  19 us
    pallas_call x6, Pallas kernels, place_piece(): pl.pallas_call(copy_into, grid_spec=pltpu.PrefetchScalarGridSpec(num_scal...  18.7 us
  transfers between devices with their start and end apart: 26, of which 13 were waited for; matrix products, arithmetic and copies ran while one was open for 7% of the time, Pallas kernels for 11%

profile of v2, /device:TPU:10, one launch (start us, length us, event | category | flops | bytes accessed | tf_op | source)
XLA Modules:
  0.0 650.8 jit_solution(5558163034339568993)
XLA Ops:
  4.9 25.3 %collective-permute-done.3 = f32[2048,128]{1,0:T(8,128)S(1)} collective-permute-done((f32[2048,128]{1,0:T(8,128)S(1)}, f32[2048,128]{1,0:T(8,128)S(1)}, u32[]{:S(2)}, u32[]{:S(2)}) %collective-permute-start.3) | collective-permute-done | bytes 1048608 | tf_op jit(solution)/shard_map/ppermute | solution.py:311
  32.2 20.6 %collective-permute-done.8 = f32[2048,128]{1,0:T(8,128)S(1)} collective-permute-done((f32[2048,128]{1,0:T(8,128)S(1)}, f32[2048,128]{1,0:T(8,128)S(1)}, u32[]{:S(2)}, u32[]{:S(2)}) %collective-permute-start.8) | collective-permute-done | bytes 1048608 | tf_op jit(solution)/shard_map/ppermute | solution.py:311
  57.9 17.4 %collective-permute-done.12 = f32[2048,128]{1,0:T(8,128)} collective-permute-done((f32[2048,128]{1,0:T(8,128)S(1)}, f32[2048,128]{1,0:T(8,128)}, u32[]{:S(2)}, u32[]{:S(2)}) %collective-permute-start.12) | collective-permute-done | bytes 1048608 | tf_op jit(solution)/shard_map/ppermute | solution.py:311
  77.6 19.1 %collective-permute-done.9 = f32[2048,128]{1,0:T(8,128)} collective-permute-done((f32[2048,128]{1,0:T(8,128)S(1)}, f32[2048,128]{1,0:T(8,128)}, u32[]{:S(2)}, u32[]{:S(2)}) %collective-permute-start.9) | collective-permute-done | bytes 1048608 | tf_op jit(solution)/shard_map/ppermute | solution.py:311
  98.9 21.5 %collective-permute-done.10 = f32[2048,128]{1,0:T(8,128)} collective-permute-done((f32[2048,128]{1,0:T(8,128)}, f32[2048,128]{1,0:T(8,128)}, u32[]{:S(2)}, u32[]{:S(2)}) %collective-permute-start.10) | collective-permute-done | bytes 1048608 | tf_op jit(solution)/shard_map/ppermute | solution.py:311
  138.2 6.1 pack.10
  150.8 57.1 %collective-permute-done.1 = f32[2,32,256]{2,1,0:T(8,128)S(1)} collective-permute-done((f32[2,32,256]{2,1,0:T(8,128)S(1)}, f32[2,32,256]{2,1,0:T(8,128)S(1)}, u32[]{:S(2)}, u32[]{:S(2)}) %collective-permute-start.1) | collective-permute-done | bytes 65568 | tf_op jit(solution)/shard_map/ppermute | solution.py:299
  207.9 36.0 %collective-permute-done.2 = f32[2,32,256]{2,1,0:T(8,128)S(1)} collective-permute-done((f32[2,32,256]{2,1,0:T(8,128)S(1)}, f32[2,32,256]{2,1,0:T(8,128)S(1)}, u32[]{:S(2)}, u32[]{:S(2)}) %collective-permute-start.2) | collective-permute-done | bytes 65568 | tf_op jit(solution)/shard_map/ppermute | solution.py:299
  256.6 7.7 %collective-permute-done.25.source = f32[1,256,4,128]{3,2,1,0:T(4,128)S(1)} collective-permute-done((f32[1,256,4,128]{3,2,1,0:T(4,128)}, f32[1,256,4,128]{3,2,1,0:T(4,128)S(1)}, u32[]{:S(2)}, u32[]{:S(2)}) %collective-permute-start.25) | collective-permute-done | bytes 524320 | tf_op jit(solution)/shard_map/ppermute | solution.py:299
  266.4 100.5 %collective-permute-done.24.source = f32[1,256,4,128]{3,2,1,0:T(4,128)S(1)} collective-permute-done((f32[1,256,4,128]{3,2,1,0:T(4,128)}, f32[1,256,4,128]{3,2,1,0:T(4,128)S(1)}, u32[]{:S(2)}, u32[]{:S(2)}) %collective-permute-start.24) | collective-permute-done | bytes 524320 | tf_op jit(solution)/shard_map/ppermute | solution.py:299
  367.4 9.9 %collective-permute-done.23.source = f32[1,256,4,128]{3,2,1,0:T(4,128)S(1)} collective-permute-done((f32[1,256,4,128]{3,2,1,0:T(4,128)}, f32[1,256,4,128]{3,2,1,0:T(4,128)S(1)}, u32[]{:S(2)}, u32[]{:S(2)}) %collective-permute-start.23) | collective-permute-done | bytes 524320 | tf_op jit(solution)/shard_map/ppermute | solution.py:299
  380.1 6.0 pack.9
  394.2 6.6 %place_own.1.__ = f32[8,4,256,4,128]{4,3,2,1,0:T(4,128)} custom-call(s32[1]{0:T(128)} %bitcast.24._, f32[16,256,4,4,128]{4,3,2,1,0:T(4,128)} %bitcast.79), custom_call_target="tpu_custom_call" | custom-call | bytes 8388608 | tf_op jit(solution)/shard_map/place_own/pallas_call | solution.py:50
  406.4 6.0 collective-permute-start.19
  416.6 39.3 %custom-call.3 = f32[2,2,128,128]{2,3,1,0:T(8,128)S(1)} custom-call(f32[2,2,128,128]{3,2,1,0:T(8,128)S(1)} %bitcast.85), custom_call_target="InvertDiagBlocksLowerTriangular" | custom-call | tf_op jit(solution)/shard_map/triangular_solve | solution.py:261
  459.1 13.6 %solve_local.1 = (f32[512,2048]{1,0:T(8,128)}, bf16[512,2048]{1,0:T(8,128)(2,1)}, bf16[512,2048]{1,0:T(8,128)(2,1)}) custom-call(f32[512,512]{1,0:T(8,128)} %select_maximum_fusion.inverse, f32[2,4096,128]{2,1,0:T(8,128)} %pad_maximum_fusion.source), custom_call_target="tpu_custom_call" | custom-call | flops 6442450944 | bytes 12582912 | tf_op jit(solution)/shard_map/solve_local/pallas_call | solution.py:177
  475.1 6.9 %place_either.1.__ = f32[8,4,256,4,128]{4,3,2,1,0:T(4,128)} custom-call(s32[2]{0:T(128)} %pad_add_fusion.at, f32[7,256,4,128]{3,2,1,0:T(4,128)} %collective-permute-done.21.one, f32[7,256,4,128]{3,2,1,0:T(4,128)} %collective-permute-done.22.other, f32[8,4,256,4,128]{4,3,2,1,0:T(4,128)} %place_solved.1._), custom_call_target="tpu_custom_call", output_to_operand_aliasing={{}: (3, {})} | custom-call | bytes 7340032 | tf_op jit(solution)/shard_map/place_either/pallas_call | solution.py:98
  482.0 6.0 place_piece.9.__
  488.0 72.4 %collective-permute-done.19.source = f32[6,256,4,128]{3,2,1,0:T(4,128)} collective-permute-done((f32[6,256,4,128]{3,2,1,0:T(4,128)}, f32[6,256,4,128]{3,2,1,0:T(4,128)}, u32[]{:S(2)}, u32[]{:S(2)}) %collective-permute-start.19) | collective-permute-done | bytes 3145760 | tf_op jit(solution)/shard_map/ppermute | solution.py:299
  565.6 5.7 collective-permute-done.18.source
  574.0 9.8 %broadcast_select_fusion = (f32[2,4096,128]{2,1,0:T(8,128)}, f32[2,4096,128]{2,1,0:T(8,128)}) fusion(pred[]{:T(512)S(6)} %eq.53, f32[2,4096,128]{2,1,0:T(8,128)} %collective-permute-done.16, f32[2,4096,128]{2,1,0:T(8,128)} %collective-permute-done.15, pred[]{:T(512)S(6)} %gt.18, f32[2,4096,128]{2,1,0:T(8,128)} %collective-permute-done.17, pred[]{:T(512)S(6)} %eq.46, ...), kind=kLoop, calls=%fused_computation.5 | loop fusion | flops 6291456 | bytes 29360132 | tf_op jit(solution)/shard_map/jit(_where)/select_n | solution.py:400
  583.8 13.8 %solve_panel.3 = (bf16[8,256,512]{2,1,0:T(8,128)(2,1)}, bf16[8,256,512]{2,1,0:T(8,128)(2,1)}) custom-call(f32[512,512]{1,0:T(8,128)} %select_maximum_fusion.inverse, f32[2,4096,128]{2,1,0:T(8,128)} %get-tuple-element.52.source), custom_call_target="tpu_custom_call" | custom-call | flops 6442450944 | bytes 8388608 | tf_op jit(solution)/shard_map/solve_panel/pallas_call | solution.py:204
  597.6 13.8 %solve_panel.2 = (bf16[8,256,512]{2,1,0:T(8,128)(2,1)}, bf16[8,256,512]{2,1,0:T(8,128)(2,1)}) custom-call(f32[512,512]{1,0:T(8,128)} %select_maximum_fusion.inverse, f32[2,4096,128]{2,1,0:T(8,128)} %get-tuple-element.53.source), custom_call_target="tpu_custom_call" | custom-call | flops 6442450944 | bytes 8388608 | tf_op jit(solution)/shard_map/solve_panel/pallas_call | solution.py:204
  611.3 39.4 %gram.1 = f32[8,2,4096,128]{3,2,1,0:T(8,128)} custom-call(bf16[8,256,512]{2,1,0:T(8,128)(2,1)} %get-tuple-element.17.refs_0_, bf16[8,256,512]{2,1,0:T(8,128)(2,1)} %get-tuple-element.18.refs_1_, bf16[8,256,512]{2,1,0:T(8,128)(2,1)} %get-tuple-element.19.refs_2_, bf16[8,256,512]{2,1,0:T(8,128)(2,1)} %get-tuple-element.20.refs_3_, ...), custom_call_target="tpu_custom_call" | custom-call | flops 25769803776 | bytes 33554432 | tf_op jit(solution)/shard_map/gram/pallas_call | solution.py:244
  (107 shorter events, 93.1 us)
Async XLA Ops:
  2.3 27.9 %collective-permute-start.3 = (f32[2048,128]{1,0:T(8,128)S(1)}, f32[2048,128]{1,0:T(8,128)S(1)}, u32[]{:S(2)}, u32[]{:S(2)}) collective-permute-start(f32[2048,128]{1,0:T(8,128)S(1)} %get-tuple-element.51), channel_id=1, source_target_pairs={{16,8},{24,16},{17,9},{25,17},{18,10},{26,18},{19,11},{27,19},{20,... | collective-permute-start | bytes 3145736 | tf_op jit(solution)/shard_map/ppermute | solution.py:311
  3.6 49.1 %collective-permute-start.8 = (f32[2048,128]{1,0:T(8,128)S(1)}, f32[2048,128]{1,0:T(8,128)S(1)}, u32[]{:S(2)}, u32[]{:S(2)}) collective-permute-start(f32[2048,128]{1,0:T(8,128)S(1)} %get-tuple-element.50), channel_id=1, source_target_pairs={{16,8},{24,16},{17,9},{25,17},{18,10},{26,18},{19,11},{27,19},{20,... | collective-permute-start | bytes 3145736 | tf_op jit(solution)/shard_map/ppermute | solution.py:311
  30.2 45.0 %collective-permute-start.12 = (f32[2048,128]{1,0:T(8,128)S(1)}, f32[2048,128]{1,0:T(8,128)}, u32[]{:S(2)}, u32[]{:S(2)}) collective-permute-start(f32[2048,128]{1,0:T(8,128)S(1)} %collective-permute-done.3), channel_id=1, source_target_pairs={{8,0},{16,8},{9,1},{17,9},{10,2},{18,10},{11,3},{19,11},{12,4},{20... | collective-permute-start | bytes 3145736 | tf_op jit(solution)/shard_map/ppermute | solution.py:311
  52.7 43.9 %collective-permute-start.9 = (f32[2048,128]{1,0:T(8,128)S(1)}, f32[2048,128]{1,0:T(8,128)}, u32[]{:S(2)}, u32[]{:S(2)}) collective-permute-start(f32[2048,128]{1,0:T(8,128)S(1)} %collective-permute-done.8), channel_id=1, source_target_pairs={{8,0},{16,8},{9,1},{17,9},{10,2},{18,10},{11,3},{19,11},{12,4},{20... | collective-permute-start | bytes 3145736 | tf_op jit(solution)/shard_map/ppermute | solution.py:311
  54.6 44.3 %collective-permute-start.11 = (f32[2048,128]{1,0:T(8,128)S(1)}, f32[2048,128]{1,0:T(8,128)}, u32[]{:S(2)}, u32[]{:S(2)}) collective-permute-start(f32[2048,128]{1,0:T(8,128)S(1)} %get-tuple-element.51), channel_id=1, source_target_pairs={{16,24},{17,25},{18,26},{19,27},{20,28},{21,29},{22,30},{23,31}} | collective-permute-start | bytes 3145736 | tf_op jit(solution)/shard_map/ppermute | solution.py:311
  56.3 42.6 %collective-permute-start.7 = (f32[2048,128]{1,0:T(8,128)S(1)}, f32[2048,128]{1,0:T(8,128)}, u32[]{:S(2)}, u32[]{:S(2)}) collective-permute-start(f32[2048,128]{1,0:T(8,128)S(1)} %get-tuple-element.50), channel_id=1, source_target_pairs={{16,24},{17,25},{18,26},{19,27},{20,28},{21,29},{22,30},{23,31}} | collective-permute-start | bytes 3145736 | tf_op jit(solution)/shard_map/ppermute | solution.py:311
  75.3 23.6 %collective-permute-start.13 = (f32[2048,128]{1,0:T(8,128)}, f32[2048,128]{1,0:T(8,128)}, u32[]{:S(2)}, u32[]{:S(2)}) collective-permute-start(f32[2048,128]{1,0:T(8,128)} %collective-permute-done.12), channel_id=1, source_target_pairs={{8,0},{9,1},{10,2},{11,3},{12,4},{13,5},{14,6},{15,7}} | collective-permute-start | bytes 3145736 | tf_op jit(solution)/shard_map/ppermute | solution.py:311
  96.6 23.7 %collective-permute-start.10 = (f32[2048,128]{1,0:T(8,128)}, f32[2048,128]{1,0:T(8,128)}, u32[]{:S(2)}, u32[]{:S(2)}) collective-permute-start(f32[2048,128]{1,0:T(8,128)} %collective-permute-done.9), channel_id=1, source_target_pairs={{8,0},{9,1},{10,2},{11,3},{12,4},{13,5},{14,6},{15,7}} | collective-permute-start | bytes 3145736 | tf_op jit(solution)/shard_map/ppermute | solution.py:311
  135.6 243.1 %collective-permute-start.15 = (f32[2,4096,128]{2,1,0:T(8,128)}, f32[2,4096,128]{2,1,0:T(8,128)}, u32[]{:S(2)}, u32[]{:S(2)}) collective-permute-start(f32[2,4096,128]{2,1,0:T(8,128)} %broadcast_select_fusion.1), channel_id=1, source_target_pairs={{0,4},{2,6},{4,0},{6,2},{9,13},{11,15},{13,9},{15,11},{16,20},{18,... | collective-permute-start | bytes 12582920 | tf_op jit(solution)/shard_map/ppermute | solution.py:377
  144.3 262.1 %collective-permute-start.21 = (f32[7,256,4,128]{3,2,1,0:T(4,128)}, f32[7,256,4,128]{3,2,1,0:T(4,128)}, u32[]{:S(2)}, u32[]{:S(2)}) collective-permute-start(f32[7,256,4,128]{3,2,1,0:T(4,128)} %pack.10), channel_id=1, source_target_pairs={{8,24},{16,0},{9,25},{17,1},{10,26},{18,2},{11,27},{19,3},{12,28},... | collective-permute-start | bytes 11010056 | tf_op jit(solution)/shard_map/ppermute | solution.py:299
  147.5 3.3 collective-permute-start
  148.1 59.7 %collective-permute-start.1 = (f32[2,32,256]{2,1,0:T(8,128)S(1)}, f32[2,32,256]{2,1,0:T(8,128)S(1)}, u32[]{:S(2)}, u32[]{:S(2)}) collective-permute-start(f32[2,32,256]{2,1,0:T(8,128)S(1)} %dynamic-slice_bitcast_fusion), channel_id=1, source_target_pairs={{16,0},{24,8},{17,1},{25,9},{18,2},{26,10},{19,3},{27,11},{20,4},{... | collective-permute-start | bytes 196616 | tf_op jit(solution)/shard_map/ppermute | solution.py:299
  149.4 94.5 %collective-permute-start.2 = (f32[2,32,256]{2,1,0:T(8,128)S(1)}, f32[2,32,256]{2,1,0:T(8,128)S(1)}, u32[]{:S(2)}, u32[]{:S(2)}) collective-permute-start(f32[2,32,256]{2,1,0:T(8,128)S(1)} %dynamic-slice_bitcast_fusion), channel_id=1, source_target_pairs={{16,8},{24,0},{17,9},{25,1},{18,10},{26,2},{19,11},{27,3},{20,12},... | collective-permute-start | bytes 196616 | tf_op jit(solution)/shard_map/ppermute | solution.py:299
  245.4 9.8 %collective-permute-start.5 = (f32[2,2,64,256]{3,2,1,0:T(8,128)S(1)}, f32[2,2,64,256]{3,2,1,0:T(8,128)S(1)}, u32[]{:S(2)}, u32[]{:S(2)}) collective-permute-start(f32[2,2,64,256]{3,2,1,0:T(8,128)S(1)} %pad_maximum_fusion.5), channel_id=1, source_target_pairs={{0,2},{1,3},{2,0},{3,1},{4,6},{5,7},{6,4},{7,5},{8,10},{9,11},{10,... | collective-permute-start | bytes 786440 | tf_op jit(solution)/shard_map/ppermute | solution.py:328
  247.4 16.9 %collective-permute-start.25 = (f32[1,256,4,128]{3,2,1,0:T(4,128)}, f32[1,256,4,128]{3,2,1,0:T(4,128)S(1)}, u32[]{:S(2)}, u32[]{:S(2)}) collective-permute-start(f32[1,256,4,128]{3,2,1,0:T(4,128)} %pack.13), channel_id=1, source_target_pairs={{0,8},{8,0},{1,9},{9,1},{2,10},{10,2},{3,11},{11,3},{4,12},{12,4},... | collective-permute-start | bytes 1572872 | tf_op jit(solution)/shard_map/ppermute | solution.py:299
  251.9 115.0 %collective-permute-start.24 = (f32[1,256,4,128]{3,2,1,0:T(4,128)}, f32[1,256,4,128]{3,2,1,0:T(4,128)S(1)}, u32[]{:S(2)}, u32[]{:S(2)}) collective-permute-start(f32[1,256,4,128]{3,2,1,0:T(4,128)} %pack.12), channel_id=1, source_target_pairs={{0,16},{8,24},{1,17},{9,25},{2,18},{10,26},{3,19},{11,27},{4,20},{... | collective-permute-start | bytes 1572872 | tf_op jit(solution)/shard_map/ppermute | solution.py:299
  255.2 122.2 %collective-permute-start.23 = (f32[1,256,4,128]{3,2,1,0:T(4,128)}, f32[1,256,4,128]{3,2,1,0:T(4,128)S(1)}, u32[]{:S(2)}, u32[]{:S(2)}) collective-permute-start(f32[1,256,4,128]{3,2,1,0:T(4,128)} %pack.11), channel_id=1, source_target_pairs={{0,24},{8,16},{1,25},{9,17},{2,26},{10,18},{3,27},{11,19},{4,28},{... | collective-permute-start | bytes 1572872 | tf_op jit(solution)/shard_map/ppermute | solution.py:299
  264.3 194.8 %collective-permute-start.22 = (f32[7,256,4,128]{3,2,1,0:T(4,128)}, f32[7,256,4,128]{3,2,1,0:T(4,128)}, u32[]{:S(2)}, u32[]{:S(2)}) collective-permute-start(f32[7,256,4,128]{3,2,1,0:T(4,128)} %pack.10), channel_id=1, source_target_pairs={{0,16},{24,8},{1,17},{25,9},{2,18},{26,10},{3,19},{27,11},{4,20},{... | collective-permute-start | bytes 11010056 | tf_op jit(solution)/shard_map/ppermute | solution.py:299
  366.9 19.3 %collective-permute-start.6 = (f32[2,2,128,256]{3,2,1,0:T(8,128)}, f32[2,2,128,256]{3,2,1,0:T(8,128)S(1)}, u32[]{:S(2)}, u32[]{:S(2)}) collective-permute-start(f32[2,2,128,256]{3,2,1,0:T(8,128)} %pad_maximum_fusion.1), channel_id=1, source_target_pairs={{0,4},{1,5},{2,6},{3,7},{4,0},{5,1},{6,2},{7,3},{8,12},{9,13},{10,... | collective-permute-start | bytes 1572872 | tf_op jit(solution)/shard_map/ppermute | solution.py:328
  377.4 196.6 %collective-permute-start.17 = (f32[2,4096,128]{2,1,0:T(8,128)}, f32[2,4096,128]{2,1,0:T(8,128)}, u32[]{:S(2)}, u32[]{:S(2)}) collective-permute-start(f32[2,4096,128]{2,1,0:T(8,128)} %broadcast_select_fusion.1), channel_id=1, source_target_pairs={{0,1},{2,3},{4,5},{6,7},{9,8},{11,10},{13,12},{15,14},{16,17},{18,... | collective-permute-start | bytes 12582920 | tf_op jit(solution)/shard_map/ppermute | solution.py:377
  378.7 195.3 %collective-permute-start.16 = (f32[2,4096,128]{2,1,0:T(8,128)}, f32[2,4096,128]{2,1,0:T(8,128)}, u32[]{:S(2)}, u32[]{:S(2)}) collective-permute-start(f32[2,4096,128]{2,1,0:T(8,128)} %collective-permute-done.15), channel_id=1, source_target_pairs={{0,1},{2,3},{4,5},{6,7},{9,8},{11,10},{13,12},{15,14},{16,17},{18,... | collective-permute-start | bytes 12582920 | tf_op jit(solution)/shard_map/ppermute | solution.py:377
  386.3 95.7 %collective-permute-start.20 = (f32[7,256,4,128]{3,2,1,0:T(4,128)}, f32[7,256,4,128]{3,2,1,0:T(4,128)}, u32[]{:S(2)}, u32[]{:S(2)}) collective-permute-start(f32[7,256,4,128]{3,2,1,0:T(4,128)} %pack.9), channel_id=1, source_target_pairs={{0,8},{8,0},{16,24},{24,16},{1,9},{9,1},{17,25},{25,17},{2,10},{10... | collective-permute-start | bytes 11010056 | tf_op jit(solution)/shard_map/ppermute | solution.py:299
  406.4 154.0 %collective-permute-start.19 = (f32[6,256,4,128]{3,2,1,0:T(4,128)}, f32[6,256,4,128]{3,2,1,0:T(4,128)}, u32[]{:S(2)}, u32[]{:S(2)}) collective-permute-start(f32[6,256,4,128]{3,2,1,0:T(4,128)} %pack.8), channel_id=1, source_target_pairs={{0,24},{8,16},{16,8},{24,0},{1,25},{9,17},{17,9},{25,1},{2,26},{10... | collective-permute-start | bytes 9437192 | tf_op jit(solution)/shard_map/ppermute | solution.py:299
  459.1 112.2 %collective-permute-start.18 = (f32[1,256,4,128]{3,2,1,0:T(4,128)S(1)}, f32[1,256,4,128]{3,2,1,0:T(4,128)S(1)}, u32[]{:S(2)}, u32[]{:S(2)}) collective-permute-start(f32[1,256,4,128]{3,2,1,0:T(4,128)S(1)} %copy-done.4), channel_id=1, source_target_pairs={{0,24},{8,16},{16,8},{24,0},{1,25},{9,17},{17,9},{25,1},{2,26},{10... | collective-permute-start | bytes 1572872 | tf_op jit(solution)/shard_map/ppermute | solution.py:299
  (12 other events, 249.3 us)

commit v3 on v2

--- a/solution.py
+++ b/solution.py
@@ -290,9 +290,9 @@
     plain_rows = [index for index in range(row_count) if index not in owners]
 
     view = working.reshape(blocks_rows, width, row_count, group, LANES)
-    slab_rows = width * columns // LANES // PARTS
-    slab_parts = working.reshape(blocks_rows, PARTS, slab_rows, LANES)
-    slab = [slab_parts[local, part] for part in range(PARTS)]
+    whole_slab = working.reshape(blocks_rows, width * columns // LANES, LANES)
+    cut = whole_slab.shape[1] * 3 // 8
+    slab = [whole_slab[local, :cut], whole_slab[local, cut:]]
 
     def shifted(value, shift, senders):
         pairs = [(index, index ^ shift) for index in senders]
@@ -317,21 +317,36 @@
 
     part = width // col_count
     slices = lax.dynamic_slice_in_dim(factor_panel[:, local, 0], col * part, part, 1)
-    heard = [slices] + [shifted(slices, shift, owners) for shift in range(1, row_count)]
-    heard, _ = lax.optimization_barrier((heard, down[-1][0]))
-    heard = jnp.stack(heard)
-    factor = jnp.stack(
-        [lax.dynamic_index_in_dim(heard, row ^ owner, 0, False) for owner in owners]
-    )
+    heard = []
+    for turn in range(1, STEPS):
+        pairs = [(owners[s], owners[(s + turn) % STEPS]) for s in range(STEPS)]
+        heard.append(lax.ppermute(slices, "row", pairs))
+    factor = []
+    for step in range(STEPS):
+        value = slices
+        for turn in range(1, STEPS):
+            value = jnp.where(row == owners[(step + turn) % STEPS], heard[turn - 1], value)
+        factor += [value[t] for t in range(step + 1)]
+    factor = jnp.stack(factor)
+    for hop in range(1, row_count):
+        pairs, ends = [], (min(owners) - hop, max(owners) + hop)
+        if ends[0] >= 0:
+            pairs.append((ends[0] + 1, ends[0]))
+        if ends[1] < row_count:
+            pairs.append((ends[1] - 1, ends[1]))
+        if not pairs:
+            break
+        moved = lax.ppermute(factor, "row", pairs)
+        factor = jnp.where((row == ends[0]) | (row == ends[1]), moved, factor)
     size = 1
     while size < col_count:
         other = lax.ppermute(factor, "col", [(index, index ^ size) for index in range(col_count)])
         swap = (col & size) > 0
-        factor = jnp.concatenate(
-            [jnp.where(swap, other, factor), jnp.where(swap, factor, other)], 2
-        )
+        factor = jnp.concatenate([jnp.where(swap, other, factor), jnp.where(swap, factor, other)], 1)
         size *= 2
-    inverse = block_inverse([[factor[s, t] for t in range(STEPS)] for s in range(STEPS)])
+    inverse = block_inverse(
+        [[factor[s * (s + 1) // 2 + t] for t in range(s + 1)] for s in range(STEPS)]
+    )
 
     def block_row(owner, part):
         value = slab[part]

time: 653 us -> 663 us (1.015)
  the two profiles are of different devices: /device:TPU:10 before, /device:TPU:0 now
where the time goes in v3:
time: 663 us; the launch traced here: 655 us
  waiting for transfers between devices  257 us (39%)
  starting transfers between devices  185 us (28%)
  Pallas kernels  140 us (21%)
  other arithmetic  60.7 us (9%)
  local copies, waits for them, and re-layouts  9.06 us (1%)
    ppermute x8, starting transfers between devices, shifted(): return lax.ppermute(value, 'row', pairs)  153 us
    ppermute x8, waiting for transfers between devices, chain(): held = lax.ppermute(held, 'row', pairs)  130 us
    ppermute x8, waiting for transfers between devices, shifted(): return lax.ppermute(value, 'row', pairs)  80.3 us
    ppermute x4, waiting for transfers between devices, joined(): return lax.ppermute(value, both, pairs)  44.4 us
    another operation x4, other arithmetic, block_inverse(): lax.linalg.triangular_solve(diagonal, eye, left_side=True, lower=True)  39.4 us
    pallas_call x1, Pallas kernels, gram_product(): pl.pallas_call(functools.partial(gram_body, panels, scale, stride, width)...  39.4 us
    pallas_call x2, Pallas kernels, solve_panel(): pl.pallas_call(functools.partial(solve_panel_body, stride, width), grid=(...  27.6 us
    pallas_call x7, Pallas kernels, pack(): pl.pallas_call(copy_block, grid_spec=pltpu.PrefetchScalarGridSpec(num_sca...  25 us
  transfers between devices with their start and end apart: 26, of which 11 were waited for; matrix products, arithmetic and copies ran while one was open for 8% of the time, Pallas kernels for 11%

profile of v3, /device:TPU:0, one launch (start us, length us, event | category | flops | bytes accessed | tf_op | source)
XLA Modules:
  0.0 654.5 jit_solution(16891874988709459577)
XLA Ops:
  8.9 75.4 %collective-permute-done.8 = f32[1536,128]{1,0:T(8,128)} collective-permute-done((f32[1536,128]{1,0:T(8,128)S(1)}, f32[1536,128]{1,0:T(8,128)}, u32[]{:S(2)}, u32[]{:S(2)}) %collective-permute-start.8) | collective-permute-done | bytes 786464 | tf_op jit(solution)/shard_map/ppermute | solution.py:311
  88.6 30.8 %collective-permute-done.9 = f32[1536,128]{1,0:T(8,128)} collective-permute-done((f32[1536,128]{1,0:T(8,128)}, f32[1536,128]{1,0:T(8,128)}, u32[]{:S(2)}, u32[]{:S(2)}) %collective-permute-start.9) | collective-permute-done | bytes 786464 | tf_op jit(solution)/shard_map/ppermute | solution.py:311
  121.7 24.1 %collective-permute-done.13 = f32[2560,128]{1,0:T(8,128)} collective-permute-done((f32[2560,128]{1,0:T(8,128)}, f32[2560,128]{1,0:T(8,128)}, u32[]{:S(2)}, u32[]{:S(2)}) %collective-permute-start.13) | collective-permute-done | bytes 1310752 | tf_op jit(solution)/shard_map/ppermute | solution.py:311
  151.6 5.4 collective-permute-start.14
  157.0 44.4 %collective-permute-done.14 = f32[2,4096,128]{2,1,0:T(8,128)} collective-permute-done((f32[2,4096,128]{2,1,0:T(8,128)}, f32[2,4096,128]{2,1,0:T(8,128)}, u32[]{:S(2)}, u32[]{:S(2)}) %collective-permute-start.14) | collective-permute-done | bytes 4194336 | tf_op jit(solution)/shard_map/ppermute | solution.py:392
  208.8 6.1 pack.10
  221.9 45.8 %collective-permute-start.25 = (f32[1,256,4,128]{3,2,1,0:T(4,128)}, f32[1,256,4,128]{3,2,1,0:T(4,128)S(1)}, u32[]{:S(2)}, u32[]{:S(2)}) collective-permute-start(f32[1,256,4,128]{3,2,1,0:T(4,128)} %pack.13), channel_id=1, source_target_pairs={{0,8},{8,0},{1,9},{9,1},{2,10},{10,2},{3,11},{11,3},{4,12},{12,4},... | collective-permute-start | bytes 1572872 | tf_op jit(solution)/shard_map/ppermute | solution.py:299
  283.5 5.0 collective-permute-done.24.source
  295.0 4.7 collective-permute-done.23.source
  300.2 6.0 pack.9
  306.2 5.4 pack.8
  313.5 6.6 %place_own.1.__ = f32[8,4,256,4,128]{4,3,2,1,0:T(4,128)} custom-call(s32[1]{0:T(128)} %bitcast.18._, f32[16,256,4,4,128]{4,3,2,1,0:T(4,128)} %bitcast.71), custom_call_target="tpu_custom_call" | custom-call | bytes 8388608 | tf_op jit(solution)/shard_map/place_own/pallas_call | solution.py:50
  320.2 96.2 %collective-permute-start.20 = (f32[7,256,4,128]{3,2,1,0:T(4,128)}, f32[7,256,4,128]{3,2,1,0:T(4,128)}, u32[]{:S(2)}, u32[]{:S(2)}) collective-permute-start(f32[7,256,4,128]{3,2,1,0:T(4,128)} %pack.9), channel_id=1, source_target_pairs={{0,8},{8,0},{16,24},{24,16},{1,9},{9,1},{17,25},{25,17},{2,10},{10... | collective-permute-start | bytes 11010056 | tf_op jit(solution)/shard_map/ppermute | solution.py:299
  430.4 39.3 %custom-call.3 = f32[2,2,128,128]{2,3,1,0:T(8,128)S(1)} custom-call(f32[2,2,128,128]{3,2,1,0:T(8,128)S(1)} %bitcast.73), custom_call_target="InvertDiagBlocksLowerTriangular" | custom-call | tf_op jit(solution)/shard_map/triangular_solve | solution.py:261
  473.4 13.4 %solve_local.1 = (f32[512,2048]{1,0:T(8,128)}, bf16[512,2048]{1,0:T(8,128)(2,1)}, bf16[512,2048]{1,0:T(8,128)(2,1)}) custom-call(f32[512,512]{1,0:T(8,128)} %select_maximum_fusion.inverse, f32[2,4096,128]{2,1,0:T(8,128)} %pad_maximum_fusion.source), custom_call_target="tpu_custom_call" | custom-call | flops 6442450944 | bytes 12582912 | tf_op jit(solution)/shard_map/solve_local/pallas_call | solution.py:177
  489.3 6.9 %place_either.1.__ = f32[8,4,256,4,128]{4,3,2,1,0:T(4,128)} custom-call(s32[2]{0:T(128)} %pad_add_fusion.at, f32[7,256,4,128]{3,2,1,0:T(4,128)} %collective-permute-done.21.one, f32[7,256,4,128]{3,2,1,0:T(4,128)} %collective-permute-done.22.other, f32[8,4,256,4,128]{4,3,2,1,0:T(4,128)} %place_solved.1._), custom_call_target="tpu_custom_call", output_to_operand_aliasing={{}: (3, {})} | custom-call | bytes 7340032 | tf_op jit(solution)/shard_map/place_either/pallas_call | solution.py:98
  496.4 6.0 place_piece.9.__
  502.4 65.2 %collective-permute-done.19.source = f32[6,256,4,128]{3,2,1,0:T(4,128)} collective-permute-done((f32[6,256,4,128]{3,2,1,0:T(4,128)}, f32[6,256,4,128]{3,2,1,0:T(4,128)}, u32[]{:S(2)}, u32[]{:S(2)}) %collective-permute-start.19) | collective-permute-done | bytes 3145760 | tf_op jit(solution)/shard_map/ppermute | solution.py:299
  567.6 5.3 place_piece.10.__
  572.9 4.5 collective-permute-done.18.source
  580.1 7.4 %broadcast_select_fusion = (f32[2,4096,128]{2,1,0:T(8,128)}, f32[2,4096,128]{2,1,0:T(8,128)}) fusion(pred[]{:T(512)S(6)} %eq.62, f32[2,4096,128]{2,1,0:T(8,128)} %collective-permute-done.16, f32[2,4096,128]{2,1,0:T(8,128)} %collective-permute-done.15, pred[]{:T(512)S(6)} %gt.18, f32[2,4096,128]{2,1,0:T(8,128)} %collective-permute-done.17, pred[]{:T(512)S(6)} %eq.60, ...), kind=kLoop, calls=%fused_computation.5 | loop fusion | flops 6291456 | bytes 29360132 | tf_op jit(solution)/shard_map/jit(_where)/select_n | solution.py:415
  587.5 13.8 %solve_panel.3 = (bf16[8,256,512]{2,1,0:T(8,128)(2,1)}, bf16[8,256,512]{2,1,0:T(8,128)(2,1)}) custom-call(f32[512,512]{1,0:T(8,128)} %select_maximum_fusion.inverse, f32[2,4096,128]{2,1,0:T(8,128)} %get-tuple-element.40.source), custom_call_target="tpu_custom_call" | custom-call | flops 6442450944 | bytes 8388608 | tf_op jit(solution)/shard_map/solve_panel/pallas_call | solution.py:204
  601.3 13.7 %solve_panel.2 = (bf16[8,256,512]{2,1,0:T(8,128)(2,1)}, bf16[8,256,512]{2,1,0:T(8,128)(2,1)}) custom-call(f32[512,512]{1,0:T(8,128)} %select_maximum_fusion.inverse, f32[2,4096,128]{2,1,0:T(8,128)} %get-tuple-element.41.source), custom_call_target="tpu_custom_call" | custom-call | flops 6442450944 | bytes 8388608 | tf_op jit(solution)/shard_map/solve_panel/pallas_call | solution.py:204
  615.1 39.4 %gram.1 = f32[8,2,4096,128]{3,2,1,0:T(8,128)} custom-call(bf16[8,256,512]{2,1,0:T(8,128)(2,1)} %get-tuple-element.9.refs_0_, bf16[8,256,512]{2,1,0:T(8,128)(2,1)} %get-tuple-element.10.refs_1_, bf16[8,256,512]{2,1,0:T(8,128)(2,1)} %get-tuple-element.11.refs_2_, bf16[8,256,512]{2,1,0:T(8,128)(2,1)} %get-tuple-element.12.refs_3_, ...), custom_call_target="tpu_custom_call" | custom-call | flops 25769803776 | bytes 33554432 | tf_op jit(solution)/shard_map/gram/pallas_call | solution.py:244
  (110 shorter events, 86.8 us)
Async XLA Ops:
  2.0 2.7 collective-permute-start.11
  4.0 2.0 collective-permute-start.7
  4.7 82.6 %collective-permute-start.12 = (f32[2560,128]{1,0:T(8,128)S(1)}, f32[2560,128]{1,0:T(8,128)}, u32[]{:S(2)}, u32[]{:S(2)}) collective-permute-start(f32[2560,128]{1,0:T(8,128)S(1)} %collective-permute-done.11), channel_id=1, source_target_pairs={{8,0},{16,8},{9,1},{17,9},{10,2},{18,10},{11,3},{19,11},{12,4},{20... | collective-permute-start | bytes 3932168 | tf_op jit(solution)/shard_map/ppermute | solution.py:311
  6.0 78.2 %collective-permute-start.8 = (f32[1536,128]{1,0:T(8,128)S(1)}, f32[1536,128]{1,0:T(8,128)}, u32[]{:S(2)}, u32[]{:S(2)}) collective-permute-start(f32[1536,128]{1,0:T(8,128)S(1)} %collective-permute-done.7), channel_id=1, source_target_pairs={{8,0},{16,8},{9,1},{17,9},{10,2},{18,10},{11,3},{19,11},{12,4},{20... | collective-permute-start | bytes 2359304 | tf_op jit(solution)/shard_map/ppermute | solution.py:311
  7.3 81.3 %collective-permute-start.6 = (f32[1536,128]{1,0:T(8,128)S(1)}, f32[1536,128]{1,0:T(8,128)}, u32[]{:S(2)}, u32[]{:S(2)}) collective-permute-start(f32[1536,128]{1,0:T(8,128)S(1)} %slice_bitcast_fusion.1), channel_id=1, source_target_pairs={{16,24},{17,25},{18,26},{19,27},{20,28},{21,29},{22,30},{23,31}} | collective-permute-start | bytes 2359304 | tf_op jit(solution)/shard_map/ppermute | solution.py:311
  84.3 35.1 %collective-permute-start.9 = (f32[1536,128]{1,0:T(8,128)}, f32[1536,128]{1,0:T(8,128)}, u32[]{:S(2)}, u32[]{:S(2)}) collective-permute-start(f32[1536,128]{1,0:T(8,128)} %collective-permute-done.8), channel_id=1, source_target_pairs={{8,0},{9,1},{10,2},{11,3},{12,4},{13,5},{14,6},{15,7}} | collective-permute-start | bytes 2359304 | tf_op jit(solution)/shard_map/ppermute | solution.py:311
  85.6 36.1 %collective-permute-start.10 = (f32[2560,128]{1,0:T(8,128)S(1)}, f32[2560,128]{1,0:T(8,128)}, u32[]{:S(2)}, u32[]{:S(2)}) collective-permute-start(f32[2560,128]{1,0:T(8,128)S(1)} %slice_bitcast_fusion), channel_id=1, source_target_pairs={{16,24},{17,25},{18,26},{19,27},{20,28},{21,29},{22,30},{23,31}} | collective-permute-start | bytes 3932168 | tf_op jit(solution)/shard_map/ppermute | solution.py:311
  87.3 58.5 %collective-permute-start.13 = (f32[2560,128]{1,0:T(8,128)}, f32[2560,128]{1,0:T(8,128)}, u32[]{:S(2)}, u32[]{:S(2)}) collective-permute-start(f32[2560,128]{1,0:T(8,128)} %collective-permute-done.12), channel_id=1, source_target_pairs={{8,0},{9,1},{10,2},{11,3},{12,4},{13,5},{14,6},{15,7}} | collective-permute-start | bytes 3932168 | tf_op jit(solution)/shard_map/ppermute | solution.py:311
  151.6 49.7 %collective-permute-start.14 = (f32[2,4096,128]{2,1,0:T(8,128)}, f32[2,4096,128]{2,1,0:T(8,128)}, u32[]{:S(2)}, u32[]{:S(2)}) collective-permute-start(f32[2,4096,128]{2,1,0:T(8,128)} %pad_maximum_fusion.source), channel_id=1, source_target_pairs={{0,2},{4,6},{9,11},{13,15},{18,16},{22,20},{27,25},{31,29}} | collective-permute-start | bytes 12582920 | tf_op jit(solution)/shard_map/ppermute | solution.py:392
  205.4 86.3 %collective-permute-start.15 = (f32[2,4096,128]{2,1,0:T(8,128)}, f32[2,4096,128]{2,1,0:T(8,128)}, u32[]{:S(2)}, u32[]{:S(2)}) collective-permute-start(f32[2,4096,128]{2,1,0:T(8,128)} %broadcast_select_fusion.1), channel_id=1, source_target_pairs={{0,4},{2,6},{4,0},{6,2},{9,13},{11,15},{13,9},{15,11},{16,20},{18,... | collective-permute-start | bytes 12582920 | tf_op jit(solution)/shard_map/ppermute | solution.py:392
  214.9 207.7 %collective-permute-start.21 = (f32[7,256,4,128]{3,2,1,0:T(4,128)}, f32[7,256,4,128]{3,2,1,0:T(4,128)}, u32[]{:S(2)}, u32[]{:S(2)}) collective-permute-start(f32[7,256,4,128]{3,2,1,0:T(4,128)} %pack.10), channel_id=1, source_target_pairs={{8,24},{16,0},{9,25},{17,1},{10,26},{18,2},{11,27},{19,3},{12,28},... | collective-permute-start | bytes 11010056 | tf_op jit(solution)/shard_map/ppermute | solution.py:299
  218.7 49.0 %collective-permute-start.2 = (f32[3,32,256]{2,1,0:T(8,128)S(1)}, f32[3,32,256]{2,1,0:T(8,128)S(1)}, u32[]{:S(2)}, u32[]{:S(2)}) collective-permute-start(f32[3,32,256]{2,1,0:T(8,128)S(1)} %broadcast_select_fusion.9), channel_id=1, source_target_pairs={{8,0},{9,1},{10,2},{11,3},{12,4},{13,5},{14,6},{15,7}} | collective-permute-start | bytes 294920 | tf_op jit(solution)/shard_map/ppermute | solution.py:339
  221.9 55.3 %collective-permute-start.25 = (f32[1,256,4,128]{3,2,1,0:T(4,128)}, f32[1,256,4,128]{3,2,1,0:T(4,128)S(1)}, u32[]{:S(2)}, u32[]{:S(2)}) collective-permute-start(f32[1,256,4,128]{3,2,1,0:T(4,128)} %pack.13), channel_id=1, source_target_pairs={{0,8},{8,0},{1,9},{9,1},{2,10},{10,2},{3,11},{11,3},{4,12},{12,4},... | collective-permute-start | bytes 1572872 | tf_op jit(solution)/shard_map/ppermute | solution.py:299
  267.8 3.3 collective-permute-start.3
  269.8 18.7 %collective-permute-start.24 = (f32[1,256,4,128]{3,2,1,0:T(4,128)}, f32[1,256,4,128]{3,2,1,0:T(4,128)S(1)}, u32[]{:S(2)}, u32[]{:S(2)}) collective-permute-start(f32[1,256,4,128]{3,2,1,0:T(4,128)} %pack.12), channel_id=1, source_target_pairs={{0,16},{8,24},{1,17},{9,25},{2,18},{10,26},{3,19},{11,27},{4,20},{... | collective-permute-start | bytes 1572872 | tf_op jit(solution)/shard_map/ppermute | solution.py:299
  271.1 9.2 %collective-permute-start.4 = (f32[3,64,256]{2,1,0:T(8,128)S(1)}, f32[3,64,256]{2,1,0:T(8,128)S(1)}, u32[]{:S(2)}, u32[]{:S(2)}) collective-permute-start(f32[3,64,256]{2,1,0:T(8,128)S(1)} %pad_maximum_fusion.4), channel_id=1, source_target_pairs={{0,2},{1,3},{2,0},{3,1},{4,6},{5,7},{6,4},{7,5},{8,10},{9,11},{10,... | collective-permute-start | bytes 589832 | tf_op jit(solution)/shard_map/ppermute | solution.py:343
  277.2 22.5 %collective-permute-start.23 = (f32[1,256,4,128]{3,2,1,0:T(4,128)}, f32[1,256,4,128]{3,2,1,0:T(4,128)S(1)}, u32[]{:S(2)}, u32[]{:S(2)}) collective-permute-start(f32[1,256,4,128]{3,2,1,0:T(4,128)} %pack.11), channel_id=1, source_target_pairs={{0,24},{8,16},{1,25},{9,17},{2,26},{10,18},{3,27},{11,19},{4,28},{... | collective-permute-start | bytes 1572872 | tf_op jit(solution)/shard_map/ppermute | solution.py:299
  280.3 192.5 %collective-permute-start.22 = (f32[7,256,4,128]{3,2,1,0:T(4,128)}, f32[7,256,4,128]{3,2,1,0:T(4,128)}, u32[]{:S(2)}, u32[]{:S(2)}) collective-permute-start(f32[7,256,4,128]{3,2,1,0:T(4,128)} %pack.10), channel_id=1, source_target_pairs={{0,16},{24,8},{1,17},{25,9},{2,18},{26,10},{3,19},{27,11},{4,20},{... | collective-permute-start | bytes 11010056 | tf_op jit(solution)/shard_map/ppermute | solution.py:299
  288.5 291.6 %collective-permute-start.17 = (f32[2,4096,128]{2,1,0:T(8,128)}, f32[2,4096,128]{2,1,0:T(8,128)}, u32[]{:S(2)}, u32[]{:S(2)}) collective-permute-start(f32[2,4096,128]{2,1,0:T(8,128)} %broadcast_select_fusion.1), channel_id=1, source_target_pairs={{0,1},{2,3},{4,5},{6,7},{9,8},{11,10},{13,12},{15,14},{16,17},{18,... | collective-permute-start | bytes 12582920 | tf_op jit(solution)/shard_map/ppermute | solution.py:392
  291.7 288.4 %collective-permute-start.16 = (f32[2,4096,128]{2,1,0:T(8,128)}, f32[2,4096,128]{2,1,0:T(8,128)}, u32[]{:S(2)}, u32[]{:S(2)}) collective-permute-start(f32[2,4096,128]{2,1,0:T(8,128)} %collective-permute-done.15), channel_id=1, source_target_pairs={{0,1},{2,3},{4,5},{6,7},{9,8},{11,10},{13,12},{15,14},{16,17},{18,... | collective-permute-start | bytes 12582920 | tf_op jit(solution)/shard_map/ppermute | solution.py:392
  299.7 20.5 %collective-permute-start.5 = (f32[3,128,256]{2,1,0:T(8,128)S(1)}, f32[3,128,256]{2,1,0:T(8,128)S(1)}, u32[]{:S(2)}, u32[]{:S(2)}) collective-permute-start(f32[3,128,256]{2,1,0:T(8,128)S(1)} %pad_maximum_fusion.1), channel_id=1, source_target_pairs={{0,4},{1,5},{2,6},{3,7},{4,0},{5,1},{6,2},{7,3},{8,12},{9,13},{10,... | collective-permute-start | bytes 1179656 | tf_op jit(solution)/shard_map/ppermute | solution.py:343
  320.2 176.2 %collective-permute-start.20 = (f32[7,256,4,128]{3,2,1,0:T(4,128)}, f32[7,256,4,128]{3,2,1,0:T(4,128)}, u32[]{:S(2)}, u32[]{:S(2)}) collective-permute-start(f32[7,256,4,128]{3,2,1,0:T(4,128)} %pack.9), channel_id=1, source_target_pairs={{0,8},{8,0},{16,24},{24,16},{1,9},{9,1},{17,25},{25,17},{2,10},{10... | collective-permute-start | bytes 11010056 | tf_op jit(solution)/shard_map/ppermute | solution.py:299
  422.6 145.1 %collective-permute-start.19 = (f32[6,256,4,128]{3,2,1,0:T(4,128)}, f32[6,256,4,128]{3,2,1,0:T(4,128)}, u32[]{:S(2)}, u32[]{:S(2)}) collective-permute-start(f32[6,256,4,128]{3,2,1,0:T(4,128)} %pack.8), channel_id=1, source_target_pairs={{0,24},{8,16},{16,8},{24,0},{1,25},{9,17},{17,9},{25,1},{2,26},{10... | collective-permute-start | bytes 9437192 | tf_op jit(solution)/shard_map/ppermute | solution.py:299
  472.9 104.6 %collective-permute-start.18 = (f32[1,256,4,128]{3,2,1,0:T(4,128)S(1)}, f32[1,256,4,128]{3,2,1,0:T(4,128)S(1)}, u32[]{:S(2)}, u32[]{:S(2)}) collective-permute-start(f32[1,256,4,128]{3,2,1,0:T(4,128)S(1)} %copy-done.4), channel_id=1, source_target_pairs={{0,24},{8,16},{16,8},{24,0},{1,25},{9,17},{17,9},{25,1},{2,26},{10... | collective-permute-start | bytes 1572872 | tf_op jit(solution)/shard_map/ppermute | solution.py:299
  (11 other events, 241.7 us)
